TPU v7x, 256 devices: a whole 4x4x8 slice. The times are simulated.
256 devices in a mesh: depth: 2 (over x_hi), mode: 2 (over x_lo), tile: 64 (over z, y, core).
Axes of the slice: x: 4 (x_hi: 2, x_lo: 2; x = x_hi * 2 + x_lo), y: 4, z: 8, core: 2. Of those that a mesh axis runs over, the one named last changes fastest.
Arguments:
- probe: float32 [2, 2, 256, 256], P('mode'), may hold values from -3 to 3
- object_slices: float32 [2, 2, 384, 16384], P('depth', None, None, 'tile'), may hold values from -4.2 to 4.2
- positions: int32 [128, 2], P('tile'), may hold values from 0 to 256, as said below
- measured: float32 [128, 256, 256], P('tile'), may hold values from 0 to 2
Outputs:
- object_gradient: float32 [2, 2, 384, 16384], P('depth', None, None, 'tile')
Inputs may be any that keep to these rules, and one draw needn't show every extreme that they name: `positions`: position r belongs to tile r // 2. Entry 0 is its window's first row, at most 128; entry 1 is its first column counted in the tile's columns extended by 128 on each side, at most 256. Windows never leave the object: in the first tile the column entry is at least 128, in the last at most 128.
All inputs are finite; a program needn't handle non-finite values.
Results may differ from a plain program's by a relative error of at most 0.0003.
Values sent between devices are 32-bit elements; how exact they have to be, the bound alone decides.
No kernel may reach another device: no remote copies, remote signals or barrier semaphores. Data moves between devices by JAX's collectives and lax.ppermute only.
A program may use at most 64 MiB of HBM per device.

v0:
```python
import numpy as np

import jax
import jax.numpy as jnp
from jax import lax
from jax.experimental import pallas as pl
from jax.experimental.pallas import tpu as pltpu
from jax.sharding import PartitionSpec as P

HALF = 128
FULL = 256
ROWS = 384
F32 = jnp.float32
BF16 = jnp.bfloat16
FS, FT, GS, GT, MS, MT, CS, CT = range(8)


def tables():
    n = np.arange(HALF)
    unit = lambda k: np.exp(-2j * np.pi * (k % FULL) / FULL) / 16.0
    even = unit(2 * n[:, None] * n[None, :])
    odd = unit(n[:, None] * (2 * n[None, :] + 1))
    j = np.arange(FULL)
    dft = unit(j[:, None] * j[None, :])
    f = np.where(j < HALF, j, j - FULL)
    h = np.exp(-2j * np.pi * (3 * f * f % 1024) / 1024)
    prop = dft.conj() @ (h[:, None] * dft)
    near, far = prop[:HALF, :HALF], prop[:HALF, HALF:]
    ms, mt = (near + far) / 2, (near - far) / 2
    pairs = lambda c: np.block([[c.real, c.imag], [-c.imag, c.real]])
    mats = [even, odd, even.conj(), odd.conj().T, ms, mt, ms.conj(), mt.conj()]
    whole = np.stack([pairs(c) for c in mats]).astype(np.float32)
    high = whole.astype(jnp.bfloat16)
    low = (whole - high.astype(np.float32)).astype(jnp.bfloat16)
    src = np.concatenate([np.arange(0, FULL, 2), np.arange(1, FULL, 2)])
    sort = np.zeros((FULL, FULL), np.float32)
    sort[src, np.arange(FULL)] = 1.0
    return high, low, sort.astype(jnp.bfloat16)


def split(x):
    high = x.astype(BF16)
    return high, (x - high.astype(F32)).astype(BF16)


def dot(a, b):
    return jnp.dot(a, b, preferred_element_type=F32)


RC = 32


def kernel(info, own_o, own_i, own_on, own_in, oth_o, oth_i, oth_on, oth_in, prb0, prb1,
           meas, kh, kl, sort, g_o, g_i, g_on, g_in,
           ext, acc, win, psi, lh, rh, mo, fld, mp, cols):
    d = info[4]
    odd = info[5]
    for blk, own, oth in ((0, own_on, oth_on), (1, own_o, oth_o), (2, own_i, oth_i), (3, own_in, oth_in)):
        at = blk + odd * (3 - 2 * blk)
        ext[d, at] = own[...]
        ext[1 - d, at] = oth[...]
    acc[...] = jnp.zeros(acc.shape, F32)
    lane = lax.broadcasted_iota(jnp.int32, (RC, HALF), 1)
    probes = (prb0, prb1)

    def put(ref, k, mode, rows, cols, value):
        high, low = split(value)
        ref[0, k, mode, rows, cols] = high
        ref[1, k, mode, rows, cols] = low

    def right(ks, kt):
        for mode in range(2):
            for k, kk in ((0, ks), (1, kt)):
                for r in range(0, FULL, HALF):
                    rr = pl.ds(r, HALF)
                    xh, xl = lh[0, k, mode, rr], lh[1, k, mode, rr]
                    mo[k, mode, rr] = dot(xh, kh[kk]) + (dot(xh, kl[kk]) + dot(xl, kh[kk]))

    def left(ks, kt, dst):
        for mode in range(2):
            for k, kk in ((0, ks), (1, kt)):
                for r in range(0, FULL, HALF):
                    rr = pl.ds(r, HALF)
                    ch, cl = kh[kk, rr], kl[kk, rr]
                    xh, xl = rh[0, k, mode], rh[1, k, mode]
                    dst[k, mode, rr] = dot(ch, xh) + (dot(cl, xh) + dot(ch, xl))

    def halves_to_lh(mode, r, ur, ui):
        rows = pl.ds(r, RC)
        a, b = ur[:, :HALF], ur[:, HALF:]
        c, e = ui[:, :HALF], ui[:, HALF:]
        put(lh, 0, mode, rows, pl.ds(0, HALF), a + b)
        put(lh, 1, mode, rows, pl.ds(0, HALF), a - b)
        put(lh, 0, mode, rows, pl.ds(HALF, HALF), c + e)
        put(lh, 1, mode, rows, pl.ds(HALF, HALF), c - e)

    def prop_middle():
        for mode in range(2):
            for r in range(0, HALF, RC):
                top, bot = pl.ds(r, RC), pl.ds(HALF + r, RC)
                pt, qt = mo[0, mode, top], mo[1, mode, top]
                pb, qb = mo[0, mode, bot], mo[1, mode, bot]
                for sign, k in ((1, 0), (-1, 1)):
                    p = pt + pb if sign > 0 else pt - pb
                    q = qt + qb if sign > 0 else qt - qb
                    y0, y1 = p + q, p - q
                    put(rh, k, mode, top, pl.ds(0, HALF), y0[:, :HALF])
                    put(rh, k, mode, top, pl.ds(HALF, HALF), y1[:, :HALF])
                    put(rh, k, mode, bot, pl.ds(0, HALF), y0[:, HALF:])
                    put(rh, k, mode, bot, pl.ds(HALF, HALF), y1[:, HALF:])

    def natural(src, mode, r):
        base = r % HALF
        top, bot = pl.ds(base, RC), pl.ds(HALF + base, RC)
        if r < HALF:
            return src[0, mode, top] + src[1, mode, top], src[0, mode, bot] + src[1, mode, bot]
        return src[0, mode, top] - src[1, mode, top], src[0, mode, bot] - src[1, mode, bot]

    def position(pos, carry):
        top = info[2 * pos]
        col = info[2 * pos + 1]
        q = jnp.where(col >= HALF, 1, 0)
        shift = col - q * HALF
        back = jnp.where(shift == 0, 0, HALF - shift)
        fwd = jnp.where(shift == HALF, 0, shift)
        keep = lane < HALF - shift
        for s in range(2):
            for c in range(2):
                for r in range(0, FULL, RC):
                    rot = [pltpu.roll(ext[s, q + b, c, pl.ds(top + r, RC), :], back, axis=1) for b in range(3)]
                    win[s, c, pl.ds(r, RC), pl.ds(0, HALF)] = jnp.where(keep, rot[0], rot[1])
                    win[s, c, pl.ds(r, RC), pl.ds(HALF, HALF)] = jnp.where(keep, rot[1], rot[2])
        for c in range(2):
            cols[c] = meas[pos, :, pl.ds(c * HALF, HALF)]
        for par in range(2):
            m = jnp.concatenate([cols[c, pl.ds(par, HALF, stride=2), :] for c in range(2)], axis=1)
            m1 = m.astype(BF16)
            rest = m - m1.astype(F32)
            m2 = rest.astype(BF16)
            m3 = (rest - m2.astype(F32)).astype(BF16)
            mp[par] = dot(m1, sort[...]) + (dot(m2, sort[...]) + dot(m3, sort[...]))
        for mode in range(2):
            for r in range(0, FULL, RC):
                rr = pl.ds(r, RC)
                pr, pi = probes[mode][0, rr], probes[mode][1, rr]
                wr, wi = win[0, 0, rr], win[0, 1, rr]
                halves_to_lh(mode, r, pr * wr - pi * wi, pr * wi + pi * wr)
        right(MS, MT)
        prop_middle()
        left(CS, CT, fld)
        for mode in range(2):
            for r in range(0, FULL, RC):
                rr = pl.ds(r, RC)
                pr, pi = natural(fld, mode, r)
                psi[mode, 0, rr] = pr
                psi[mode, 1, rr] = pi
                wr, wi = win[1, 0, rr], win[1, 1, rr]
                halves_to_lh(mode, r, pr * wr - pi * wi, pr * wi + pi * wr)
        right(FS, FT)
        for mode in range(2):
            for r in range(0, HALF, RC):
                tp, bt = pl.ds(r, RC), pl.ds(HALF + r, RC)
                for c in range(2):
                    et, eb = mo[c, mode, tp], mo[c, mode, bt]
                    s, t = et + eb, et - eb
                    at = pl.ds(c * HALF, HALF)
                    put(rh, 0, mode, tp, at, s[:, :HALF])
                    put(rh, 0, mode, bt, at, s[:, HALF:])
                    put(rh, 1, mode, tp, at, t[:, :HALF])
                    put(rh, 1, mode, bt, at, t[:, HALF:])
        left(GS, GT, fld)
        for par in range(2):
            for r in range(0, HALF, RC):
                tp, bt = pl.ds(r, RC), pl.ds(HALF + r, RC)
                fr = [fld[par, mode, tp] for mode in range(2)]
                fi = [fld[par, mode, bt] for mode in range(2)]
                resid = (fr[0] * fr[0] + fi[0] * fi[0]) + (fr[1] * fr[1] + fi[1] * fi[1]) - mp[par, tp]
                for mode in range(2):
                    put(rh, par, mode, tp, slice(None), resid * fr[mode])
                    put(rh, par, mode, bt, slice(None), resid * fi[mode])
        left(FS, FT, fld)
        for mode in range(2):
            for r in range(0, FULL, RC):
                rr = pl.ds(r, RC)
                xr, xi = natural(fld, mode, r)
                put(lh, 0, mode, rr, pl.ds(0, HALF), xr[:, :HALF])
                put(lh, 0, mode, rr, pl.ds(HALF, HALF), xi[:, :HALF])
                put(lh, 1, mode, rr, pl.ds(0, HALF), xr[:, HALF:])
                put(lh, 1, mode, rr, pl.ds(HALF, HALF), xi[:, HALF:])
        right(GS, GT)

        def wave_back(mode, rr):
            p, q_ = mo[0, mode, rr], mo[1, mode, rr]
            y0, y1 = p + q_, p - q_
            qr = jnp.concatenate([y0[:, :HALF], y1[:, :HALF]], axis=1)
            qi = jnp.concatenate([y0[:, HALF:], y1[:, HALF:]], axis=1)
            return qr, qi

        @pl.when(d == 0)
        def _():
            for mode in range(2):
                for r in range(0, FULL, RC):
                    rr = pl.ds(r, RC)
                    qr, qi = wave_back(mode, rr)
                    wr, wi = win[1, 0, rr], win[1, 1, rr]
                    halves_to_lh(mode, r, wr * qr + wi * qi, wr * qi - wi * qr)
            right(CS, CT)
            prop_middle()
            left(MS, MT, fld)
            for r in range(0, FULL, RC):
                rr = pl.ds(r, RC)
                vr = vi = None
                for mode in range(2):
                    qr, qi = natural(fld, mode, r)
                    pr, pi = probes[mode][0, rr], probes[mode][1, rr]
                    ar, ai = pr * qr + pi * qi, pr * qi - pi * qr
                    vr, vi = (ar, ai) if vr is None else (vr + ar, vi + ai)
                win[0, 0, rr] = vr
                win[0, 1, rr] = vi

        @pl.when(d != 0)
        def _():
            for r in range(0, FULL, RC):
                rr = pl.ds(r, RC)
                vr = vi = None
                for mode in range(2):
                    qr, qi = wave_back(mode, rr)
                    pr, pi = psi[mode, 0, rr], psi[mode, 1, rr]
                    ar, ai = pr * qr + pi * qi, pr * qi - pi * qr
                    vr, vi = (ar, ai) if vr is None else (vr + ar, vi + ai)
                win[0, 0, rr] = vr
                win[0, 1, rr] = vi

        later = lane >= shift
        zero = jnp.zeros((RC, HALF), F32)
        for c in range(2):
            for r in range(0, FULL, RC):
                rr = pl.ds(r, RC)
                r0 = pltpu.roll(win[0, c, rr, pl.ds(0, HALF)], fwd, axis=1)
                r1 = pltpu.roll(win[0, c, rr, pl.ds(HALF, HALF)], fwd, axis=1)
                vals = (jnp.where(later, r0, zero), jnp.where(later, r1, r0), jnp.where(later, zero, r1))
                for b in range(3):
                    acc[q + b, c, pl.ds(top + r, RC), :] = acc[q + b, c, pl.ds(top + r, RC), :] + vals[b]
        return carry

    lax.fori_loop(0, 2, position, 0)
    for blk, out in ((0, g_on), (1, g_o), (2, g_i), (3, g_in)):
        out[...] = acc[blk + odd * (3 - 2 * blk)]


def merge(flag, a, b, ra, rb, out):
    odd = flag[5]
    out[0, :, :, pl.ds(pl.multiple_of(odd * HALF, HALF), HALF)] = a[...] + ra[...]
    out[0, :, :, pl.ds(pl.multiple_of((1 - odd) * HALF, HALF), HALF)] = b[...] + rb[...]


def body(probe, object_slices, positions, measured):
    d = lax.axis_index("depth")
    m = lax.axis_index("mode")
    t = lax.axis_index("tile")
    tiles = lax.axis_size("tile")
    odd = t % 2
    cross = [(0, 3), (3, 0), (1, 2), (2, 1)]
    pair = [(i, i ^ 1) for i in range(tiles)]
    side = [(i, i + 1) for i in range(1, tiles - 1, 2)]
    side = side + [(j, i) for i, j in side]
    o = object_slices[0]
    lft, rgt = o[..., :HALF], o[..., HALF:]
    own_o = jnp.where(odd == 0, lft, rgt)
    own_i = jnp.where(odd == 0, rgt, lft)
    oth_o = lax.ppermute(own_o, ("depth", "mode"), cross)
    oth_i = lax.ppermute(own_i, ("depth", "mode"), cross)
    own_on = lax.ppermute(own_o, "tile", side)
    own_in = lax.ppermute(own_i, "tile", pair)
    prb = lax.ppermute(probe, "mode", [(0, 1), (1, 0)])
    oth_on = lax.ppermute(oth_o, "tile", side)
    oth_in = lax.ppermute(oth_i, "tile", pair)
    info = jnp.concatenate([positions.reshape(-1), jnp.stack([d, odd]).astype(jnp.int32)])
    high, low, sort = tables()
    blk = jax.ShapeDtypeStruct((2, ROWS, HALF), F32)
    smem = pl.BlockSpec(memory_space=pltpu.SMEM)
    vmem = pl.BlockSpec(memory_space=pltpu.VMEM)
    g_o, g_i, g_on, g_in = pl.pallas_call(
        kernel,
        out_shape=(blk,) * 4,
        in_specs=[smem] + [vmem] * 14,
        out_specs=(vmem,) * 4,
        scratch_shapes=[
            pltpu.VMEM((2, 4, 2, ROWS, HALF), F32),
            pltpu.VMEM((4, 2, ROWS, HALF), F32),
            pltpu.VMEM((2, 2, FULL, FULL), F32),
            pltpu.VMEM((2, 2, FULL, FULL), F32),
            pltpu.VMEM((2, 2, 2, FULL, FULL), BF16),
            pltpu.VMEM((2, 2, 2, FULL, FULL), BF16),
            pltpu.VMEM((2, 2, FULL, FULL), F32),
            pltpu.VMEM((2, 2, FULL, FULL), F32),
            pltpu.VMEM((2, HALF, FULL), F32),
            pltpu.VMEM((2, FULL, HALF), F32),
        ],
        name="grad",
    )(info, own_o, own_i, own_on, own_in, oth_o, oth_i, oth_on, oth_in, probe[0], prb[0],
      measured, jnp.asarray(high), jnp.asarray(low), jnp.asarray(sort))
    r_o = lax.ppermute(g_on, "tile", side)
    r_i = lax.ppermute(g_in, "tile", pair)
    return pl.pallas_call(
        merge,
        out_shape=jax.ShapeDtypeStruct((1, 2, ROWS, FULL), F32),
        in_specs=[smem] + [vmem] * 4,
        out_specs=vmem,
        name="merge",
    )(info, g_o, g_i, r_o, r_i)


def solution(mesh):
    placed = (
        P("mode", None, None, None),
        P("depth", None, None, "tile"),
        P("tile", None),
        P("tile", None, None),
    )
    return jax.shard_map(
        body, mesh=mesh, in_specs=placed, out_specs=P("depth", None, None, "tile"), check_vma=False
    )
```

profile of v0, /device:TPU:128, one launch (start us, length us, event | category | flops | bytes accessed | tf_op | source)
XLA Modules:
  0.0 65.1 jit_solution(15741295804410763193)
XLA Ops:
  0.0 1.2 %slice_select_fusion = (f32[2,384,128]{2,1,0:T(8,128)S(1)}, f32[2,384,128]{2,1,0:T(8,128)S(1)}) fusion(f32[2,384,256]{2,1,0:T(8,128)} %bitcast.5, pred[]{:T(512)S(6)} %eq.6), kind=kLoop, calls=%fused_computation | loop fusion | flops 196608 | bytes 1572865 | tf_op jit(solution)/shard_map/jit(_where)/select_n | solution.py:270
  1.3 2.8 %collective-permute-start.3 = (f32[2,384,128]{2,1,0:T(8,128)S(1)}, f32[2,384,128]{2,1,0:T(8,128)S(1)}, u32[]{:S(2)}, u32[]{:S(2)}) collective-permute-start(f32[2,384,128]{2,1,0:T(8,128)S(1)} %get-tuple-element.13.own_i), channel_id=1, source_target_pairs={{0,192},{192,0},{64,128},{128,64},{1,193},{193,1},{65,129},{129,65... | collective-permute-start | bytes 1179656 | tf_op jit(solution)/shard_map/ppermute | solution.py:272
  4.1 0.5 collective-permute-start.2
  4.6 0.3 collective-permute-start.6
  4.9 4.6 %collective-permute-start = (f32[2,384,128]{2,1,0:T(8,128)S(1)}, f32[2,384,128]{2,1,0:T(8,128)S(1)}, u32[]{:S(2)}, u32[]{:S(2)}) collective-permute-start(f32[2,384,128]{2,1,0:T(8,128)S(1)} %get-tuple-element.14.own_o), channel_id=1, source_target_pairs={{1,2},{3,4},{5,6},{7,8},{9,10},{11,12},{13,14},{15,16},{17,18},{19... | collective-permute-start | bytes 1179656 | tf_op jit(solution)/shard_map/ppermute | solution.py:273
  9.4 5.1 %collective-permute-done.3.oth_i = f32[2,384,128]{2,1,0:T(8,128)S(1)} collective-permute-done((f32[2,384,128]{2,1,0:T(8,128)S(1)}, f32[2,384,128]{2,1,0:T(8,128)S(1)}, u32[]{:S(2)}, u32[]{:S(2)}) %collective-permute-start.3) | collective-permute-done | bytes 393248 | tf_op jit(solution)/shard_map/ppermute | solution.py:272
  14.5 0.0 collective-permute-start.5
  14.5 7.3 %collective-permute-done.2.oth_o = f32[2,384,128]{2,1,0:T(8,128)S(1)} collective-permute-done((f32[2,384,128]{2,1,0:T(8,128)S(1)}, f32[2,384,128]{2,1,0:T(8,128)S(1)}, u32[]{:S(2)}, u32[]{:S(2)}) %collective-permute-start.2) | collective-permute-done | bytes 393248 | tf_op jit(solution)/shard_map/ppermute | solution.py:271
  21.8 3.0 %collective-permute-start.4 = (f32[2,384,128]{2,1,0:T(8,128)S(1)}, f32[2,384,128]{2,1,0:T(8,128)}, u32[]{:S(2)}, u32[]{:S(2)}) collective-permute-start(f32[2,384,128]{2,1,0:T(8,128)S(1)} %collective-permute-done.2.oth_o), channel_id=1, source_target_pairs={{1,2},{3,4},{5,6},{7,8},{9,10},{11,12},{13,14},{15,16},{17,18},{19... | collective-permute-start | bytes 1179656 | tf_op jit(solution)/shard_map/ppermute | solution.py:276
  24.9 0.0 copy-start.10
  24.9 0.7 %copy-done.10 = s32[2,2]{1,0:T(2,128)S(1)} copy-done((s32[2,2]{1,0:T(2,128)S(1)}, s32[2,2]{1,0:T(2,128)}, u32[]{:S(2)}) %copy-start.10) | copy-done | bytes 40
  25.6 0.1 reshape.3
  25.7 0.6 pad_add_fusion.info.flag
  26.3 0.0 collective-permute-done.own_on
  26.3 0.0 collective-permute-done.6
  26.3 0.0 copy-start.3
  26.3 8.0 %collective-permute-done.4.oth_on = f32[2,384,128]{2,1,0:T(8,128)} collective-permute-done((f32[2,384,128]{2,1,0:T(8,128)S(1)}, f32[2,384,128]{2,1,0:T(8,128)}, u32[]{:S(2)}, u32[]{:S(2)}) %collective-permute-start.4) | collective-permute-done | bytes 393248 | tf_op jit(solution)/shard_map/ppermute | solution.py:276
  34.4 14.9 %grad.1 = (f32[2,384,128]{2,1,0:T(8,128)}, f32[2,384,128]{2,1,0:T(8,128)}, f32[2,384,128]{2,1,0:T(8,128)}, f32[2,384,128]{2,1,0:T(8,128)}) custom-call(s32[6]{0:T(128)} %pad_add_fusion.info.flag, f32[2,384,128]{2,1,0:T(8,128)} %copy-done.1, f32[2,384,128]{2,1,0:T(8,128)} %copy-done, f32[2,384,128]{2,1,0:T(8,128)} %copy-done.7, f32[2,384,128]{2,1,0:T(8,128)} %copy-done.6, ...), custom_call_target="tpu_custom_call" | custom-call | tf_op jit(solution)/shard_map/grad/pallas_call | solution.py:283
  49.3 3.1 %collective-permute-start.7 = (f32[2,384,128]{2,1,0:T(8,128)}, f32[2,384,128]{2,1,0:T(8,128)S(1)}, u32[]{:S(2)}, u32[]{:S(2)}) collective-permute-start(f32[2,384,128]{2,1,0:T(8,128)} %get-tuple-element.11), channel_id=1, source_target_pairs={{1,2},{3,4},{5,6},{7,8},{9,10},{11,12},{13,14},{15,16},{17,18},{19... | collective-permute-start | bytes 1179656 | tf_op jit(solution)/shard_map/ppermute | solution.py:303
  52.4 0.1 collective-permute-start.8
  52.5 9.4 %collective-permute-done.7.ra = f32[2,384,128]{2,1,0:T(8,128)S(1)} collective-permute-done((f32[2,384,128]{2,1,0:T(8,128)}, f32[2,384,128]{2,1,0:T(8,128)S(1)}, u32[]{:S(2)}, u32[]{:S(2)}) %collective-permute-start.7) | collective-permute-done | bytes 393248 | tf_op jit(solution)/shard_map/ppermute | solution.py:303
  61.9 0.7 %copy-done.8 = f32[2,384,128]{2,1,0:T(8,128)} copy-done((f32[2,384,128]{2,1,0:T(8,128)}, f32[2,384,128]{2,1,0:T(8,128)S(1)}, u32[]{:S(2)}) %copy-start.8) | copy-done | bytes 393240
  62.6 0.1 copy-done.9
  62.8 2.3 %merge.1 = f32[1,2,384,256]{3,2,1,0:T(8,128)} custom-call(s32[6]{0:T(128)} %pad_add_fusion.info.flag, f32[2,384,128]{2,1,0:T(8,128)} %get-tuple-element.9.a, f32[2,384,128]{2,1,0:T(8,128)} %get-tuple-element.10.b, f32[2,384,128]{2,1,0:T(8,128)} %copy-done.8, f32[2,384,128]{2,1,0:T(8,128)} %copy-done.9), custom_call_target="tpu_custom_call" | custom-call | tf_op jit(solution)/shard_map/merge/pallas_call | solution.py:305
  (21 shorter events, 0.0 us)
Async XLA Ops:
  0.0 4.6 %copy-start.2 = (f32[1,2,256,256]{3,2,1,0:T(8,128)S(1)}, f32[1,2,256,256]{3,2,1,0:T(8,128)}, u32[]{:S(2)}) copy-start(f32[1,2,256,256]{3,2,1,0:T(8,128)} %param.7) | copy-start | bytes 1572868
  1.2 33.1 %copy-start = (f32[2,384,128]{2,1,0:T(8,128)}, f32[2,384,128]{2,1,0:T(8,128)S(1)}, u32[]{:S(2)}) copy-start(f32[2,384,128]{2,1,0:T(8,128)S(1)} %get-tuple-element.13.own_i) | copy-start | bytes 1179652
  1.2 33.1 %copy-start.1 = (f32[2,384,128]{2,1,0:T(8,128)}, f32[2,384,128]{2,1,0:T(8,128)S(1)}, u32[]{:S(2)}) copy-start(f32[2,384,128]{2,1,0:T(8,128)S(1)} %get-tuple-element.14.own_o) | copy-start | bytes 1179652
  1.3 13.3 %collective-permute-start.3 = (f32[2,384,128]{2,1,0:T(8,128)S(1)}, f32[2,384,128]{2,1,0:T(8,128)S(1)}, u32[]{:S(2)}, u32[]{:S(2)}) collective-permute-start(f32[2,384,128]{2,1,0:T(8,128)S(1)} %get-tuple-element.13.own_i), channel_id=1, source_target_pairs={{0,192},{192,0},{64,128},{128,64},{1,193},{193,1},{65,129},{129,65... | collective-permute-start | bytes 1179656 | tf_op jit(solution)/shard_map/ppermute | solution.py:272
  4.1 17.7 %collective-permute-start.2 = (f32[2,384,128]{2,1,0:T(8,128)S(1)}, f32[2,384,128]{2,1,0:T(8,128)S(1)}, u32[]{:S(2)}, u32[]{:S(2)}) collective-permute-start(f32[2,384,128]{2,1,0:T(8,128)S(1)} %get-tuple-element.14.own_o), channel_id=1, source_target_pairs={{0,192},{192,0},{64,128},{128,64},{1,193},{193,1},{65,129},{129,65... | collective-permute-start | bytes 1179656 | tf_op jit(solution)/shard_map/ppermute | solution.py:271
  4.6 21.7 %collective-permute-start.6 = (f32[1,2,256,256]{3,2,1,0:T(8,128)S(1)}, f32[1,2,256,256]{3,2,1,0:T(8,128)S(1)}, u32[]{:S(2)}, u32[]{:S(2)}) collective-permute-start(f32[1,2,256,256]{3,2,1,0:T(8,128)S(1)} %copy-done.2), channel_id=1, source_target_pairs={{0,64},{64,0},{1,65},{65,1},{2,66},{66,2},{3,67},{67,3},{4,68},{68... | collective-permute-start | bytes 1572872 | tf_op jit(solution)/shard_map/ppermute | solution.py:275
  4.9 21.4 %collective-permute-start.1 = (f32[2,384,128]{2,1,0:T(8,128)S(1)}, f32[2,384,128]{2,1,0:T(8,128)S(1)}, u32[]{:S(2)}, u32[]{:S(2)}) collective-permute-start(f32[2,384,128]{2,1,0:T(8,128)S(1)} %get-tuple-element.13.own_i), channel_id=1, source_target_pairs={{0,1},{1,0},{2,3},{3,2},{4,5},{5,4},{6,7},{7,6},{8,9},{9,8},{10,11... | collective-permute-start | bytes 1179656 | tf_op jit(solution)/shard_map/ppermute | solution.py:274
  4.9 21.4 %collective-permute-start = (f32[2,384,128]{2,1,0:T(8,128)S(1)}, f32[2,384,128]{2,1,0:T(8,128)S(1)}, u32[]{:S(2)}, u32[]{:S(2)}) collective-permute-start(f32[2,384,128]{2,1,0:T(8,128)S(1)} %get-tuple-element.14.own_o), channel_id=1, source_target_pairs={{1,2},{3,4},{5,6},{7,8},{9,10},{11,12},{13,14},{15,16},{17,18},{19... | collective-permute-start | bytes 1179656 | tf_op jit(solution)/shard_map/ppermute | solution.py:273
  14.5 19.8 %copy-start.4 = (f32[2,384,128]{2,1,0:T(8,128)}, f32[2,384,128]{2,1,0:T(8,128)S(1)}, u32[]{:S(2)}) copy-start(f32[2,384,128]{2,1,0:T(8,128)S(1)} %collective-permute-done.3.oth_i) | copy-start | bytes 1179652
  14.5 11.8 %collective-permute-start.5 = (f32[2,384,128]{2,1,0:T(8,128)S(1)}, f32[2,384,128]{2,1,0:T(8,128)}, u32[]{:S(2)}, u32[]{:S(2)}) collective-permute-start(f32[2,384,128]{2,1,0:T(8,128)S(1)} %collective-permute-done.3.oth_i), channel_id=1, source_target_pairs={{0,1},{1,0},{2,3},{3,2},{4,5},{5,4},{6,7},{7,6},{8,9},{9,8},{10,11... | collective-permute-start | bytes 1179656 | tf_op jit(solution)/shard_map/ppermute | solution.py:277
  21.8 12.5 %copy-start.5 = (f32[2,384,128]{2,1,0:T(8,128)}, f32[2,384,128]{2,1,0:T(8,128)S(1)}, u32[]{:S(2)}) copy-start(f32[2,384,128]{2,1,0:T(8,128)S(1)} %collective-permute-done.2.oth_o) | copy-start | bytes 1179652
  21.8 12.5 %collective-permute-start.4 = (f32[2,384,128]{2,1,0:T(8,128)S(1)}, f32[2,384,128]{2,1,0:T(8,128)}, u32[]{:S(2)}, u32[]{:S(2)}) collective-permute-start(f32[2,384,128]{2,1,0:T(8,128)S(1)} %collective-permute-done.2.oth_o), channel_id=1, source_target_pairs={{1,2},{3,4},{5,6},{7,8},{9,10},{11,12},{13,14},{15,16},{17,18},{19... | collective-permute-start | bytes 1179656 | tf_op jit(solution)/shard_map/ppermute | solution.py:276
  24.9 0.7 %copy-start.10 = (s32[2,2]{1,0:T(2,128)S(1)}, s32[2,2]{1,0:T(2,128)}, u32[]{:S(2)}) copy-start(s32[2,2]{1,0:T(2,128)} %param.9) | copy-start | bytes 52
  26.3 8.1 %copy-start.6 = (f32[2,384,128]{2,1,0:T(8,128)}, f32[2,384,128]{2,1,0:T(8,128)S(1)}, u32[]{:S(2)}) copy-start(f32[2,384,128]{2,1,0:T(8,128)S(1)} %collective-permute-done.1.own_in) | copy-start | bytes 1179652
  26.3 8.1 %copy-start.7 = (f32[2,384,128]{2,1,0:T(8,128)}, f32[2,384,128]{2,1,0:T(8,128)S(1)}, u32[]{:S(2)}) copy-start(f32[2,384,128]{2,1,0:T(8,128)S(1)} %collective-permute-done.own_on) | copy-start | bytes 1179652
  26.3 8.1 %copy-start.3 = (f32[1,2,256,256]{3,2,1,0:T(8,128)}, f32[1,2,256,256]{3,2,1,0:T(8,128)S(1)}, u32[]{:S(2)}) copy-start(f32[1,2,256,256]{3,2,1,0:T(8,128)S(1)} %collective-permute-done.6) | copy-start | bytes 1572868
  49.3 12.6 %collective-permute-start.7 = (f32[2,384,128]{2,1,0:T(8,128)}, f32[2,384,128]{2,1,0:T(8,128)S(1)}, u32[]{:S(2)}, u32[]{:S(2)}) collective-permute-start(f32[2,384,128]{2,1,0:T(8,128)} %get-tuple-element.11), channel_id=1, source_target_pairs={{1,2},{3,4},{5,6},{7,8},{9,10},{11,12},{13,14},{15,16},{17,18},{19... | collective-permute-start | bytes 1179656 | tf_op jit(solution)/shard_map/ppermute | solution.py:303
  52.4 9.5 %collective-permute-start.8 = (f32[2,384,128]{2,1,0:T(8,128)}, f32[2,384,128]{2,1,0:T(8,128)S(1)}, u32[]{:S(2)}, u32[]{:S(2)}) collective-permute-start(f32[2,384,128]{2,1,0:T(8,128)} %get-tuple-element.12), channel_id=1, source_target_pairs={{0,1},{1,0},{2,3},{3,2},{4,5},{5,4},{6,7},{7,6},{8,9},{9,8},{10,11... | collective-permute-start | bytes 1179656 | tf_op jit(solution)/shard_map/ppermute | solution.py:304
  61.9 0.8 %copy-start.8 = (f32[2,384,128]{2,1,0:T(8,128)}, f32[2,384,128]{2,1,0:T(8,128)S(1)}, u32[]{:S(2)}) copy-start(f32[2,384,128]{2,1,0:T(8,128)S(1)} %collective-permute-done.7.ra) | copy-start | bytes 1179652
  61.9 0.9 %copy-start.9 = (f32[2,384,128]{2,1,0:T(8,128)}, f32[2,384,128]{2,1,0:T(8,128)S(1)}, u32[]{:S(2)}) copy-start(f32[2,384,128]{2,1,0:T(8,128)S(1)} %collective-permute-done.8.rb) | copy-start | bytes 1179652
where the time goes:
time: 65.3 us; the launch traced here: 65.1 us
  waiting for transfers between devices  29.8 us (46%)
  Pallas kernels  17.2 us (26%)
  starting transfers between devices  14.4 us (22%)
  other arithmetic  1.86 us (3%)
  local copies, waits for them, and re-layouts  1.66 us (3%)
    pallas_call x1, Pallas kernels, body(): pl.pallas_call(kernel, out_shape=(blk,) * 4, in_specs=[smem] + [vmem] * 1...  14.9 us
    ppermute x1, waiting for transfers between devices, body(): r_o = lax.ppermute(g_on, 'tile', side)  9.43 us
    ppermute x1, waiting for transfers between devices, body(): oth_on = lax.ppermute(oth_o, 'tile', side)  8 us
    ppermute x1, waiting for transfers between devices, body(): oth_o = lax.ppermute(own_o, ('depth', 'mode'), cross)  7.29 us
    ppermute x1, waiting for transfers between devices, body(): oth_i = lax.ppermute(own_i, ('depth', 'mode'), cross)  5.1 us
    ppermute x1, starting transfers between devices, body(): own_on = lax.ppermute(own_o, 'tile', side)  4.57 us
    ppermute x1, starting transfers between devices, body(): r_o = lax.ppermute(g_on, 'tile', side)  3.08 us
    ppermute x1, starting transfers between devices, body(): oth_on = lax.ppermute(oth_o, 'tile', side)  3.04 us
  transfers between devices with their start and end apart: 9, of which 4 were waited for; matrix products, arithmetic and copies ran while one was open for 1% of the time, Pallas kernels for 0%

commit v1 on v0

v1 whole, which is shorter than its diff:
```python
import numpy as np

import jax
import jax.numpy as jnp
from jax import lax
from jax.experimental import pallas as pl
from jax.experimental.pallas import tpu as pltpu
from jax.sharding import PartitionSpec as P


HALF = 128
FULL = 256
ROWS = 384
F32 = jnp.float32
BF16 = jnp.bfloat16
FS, FT, GS, GT, MS, MT, CS, CT = range(8)


def tables():
    n = np.arange(HALF)
    unit = lambda k: np.exp(-2j * np.pi * (k % FULL) / FULL) / 16.0
    even = unit(2 * n[:, None] * n[None, :])
    odd = unit(n[:, None] * (2 * n[None, :] + 1))
    j = np.arange(FULL)
    dft = unit(j[:, None] * j[None, :])
    f = np.where(j < HALF, j, j - FULL)
    h = np.exp(-2j * np.pi * (3 * f * f % 1024) / 1024)
    prop = dft.conj() @ (h[:, None] * dft)
    near, far = prop[:HALF, :HALF], prop[:HALF, HALF:]
    ms, mt = (near + far) / 2, (near - far) / 2
    pairs = lambda c: np.block([[c.real, c.imag], [-c.imag, c.real]])
    mats = [even, odd, even.conj(), odd.conj().T, ms, mt, ms.conj(), mt.conj()]
    whole = np.stack([pairs(c) for c in mats]).astype(np.float32)
    high = whole.astype(jnp.bfloat16)
    low = (whole - high.astype(np.float32)).astype(jnp.bfloat16)
    src = np.concatenate([np.arange(0, FULL, 2), np.arange(1, FULL, 2)])
    sort = np.zeros((FULL, FULL), np.float32)
    sort[src, np.arange(FULL)] = 1.0
    return high, low, sort.astype(jnp.bfloat16)


def split(x):
    high = x.astype(BF16)
    return high, (x - high.astype(F32)).astype(BF16)


def dot(a, b):
    return jnp.dot(a, b, preferred_element_type=F32)


RC = 32
LIMIT = 20 * 2**20


def put(ref, k, mode, rows, cols, value):
    high, low = split(value)
    ref[0, k, mode, rows, cols] = high
    ref[1, k, mode, rows, cols] = low


def right(lh, mo, kh, kl, ks, kt):
    for mode in range(2):
        for k, kk in ((0, ks), (1, kt)):
            for r in range(0, FULL, HALF):
                rr = pl.ds(r, HALF)
                xh, xl = lh[0, k, mode, rr], lh[1, k, mode, rr]
                mo[k, mode, rr] = dot(xh, kh[kk]) + (dot(xh, kl[kk]) + dot(xl, kh[kk]))


def left(rh, dst, kh, kl, ks, kt):
    for mode in range(2):
        for k, kk in ((0, ks), (1, kt)):
            for r in range(0, FULL, HALF):
                rr = pl.ds(r, HALF)
                ch, cl = kh[kk, rr], kl[kk, rr]
                xh, xl = rh[0, k, mode], rh[1, k, mode]
                dst[k, mode, rr] = dot(ch, xh) + (dot(cl, xh) + dot(ch, xl))


def halves_to_lh(lh, mode, r, ur, ui):
    rows = pl.ds(r, RC)
    a, b = ur[:, :HALF], ur[:, HALF:]
    c, e = ui[:, :HALF], ui[:, HALF:]
    put(lh, 0, mode, rows, pl.ds(0, HALF), a + b)
    put(lh, 1, mode, rows, pl.ds(0, HALF), a - b)
    put(lh, 0, mode, rows, pl.ds(HALF, HALF), c + e)
    put(lh, 1, mode, rows, pl.ds(HALF, HALF), c - e)


def prop_middle(mo, rh):
    for mode in range(2):
        for r in range(0, HALF, RC):
            top, bot = pl.ds(r, RC), pl.ds(HALF + r, RC)
            pt, qt = mo[0, mode, top], mo[1, mode, top]
            pb, qb = mo[0, mode, bot], mo[1, mode, bot]
            for sign, k in ((1, 0), (-1, 1)):
                p = pt + pb if sign > 0 else pt - pb
                q = qt + qb if sign > 0 else qt - qb
                y0, y1 = p + q, p - q
                put(rh, k, mode, top, pl.ds(0, HALF), y0[:, :HALF])
                put(rh, k, mode, top, pl.ds(HALF, HALF), y1[:, :HALF])
                put(rh, k, mode, bot, pl.ds(0, HALF), y0[:, HALF:])
                put(rh, k, mode, bot, pl.ds(HALF, HALF), y1[:, HALF:])


def natural(src, mode, r):
    base = r % HALF
    top, bot = pl.ds(base, RC), pl.ds(HALF + base, RC)
    if r < HALF:
        return src[0, mode, top] + src[1, mode, top], src[0, mode, bot] + src[1, mode, bot]
    return src[0, mode, top] - src[1, mode, top], src[0, mode, bot] - src[1, mode, bot]


def place(info, pos):
    top = info[pos, 0]
    col = info[pos, 1]
    q = jnp.where(col >= HALF, 1, 0)
    return top, q, col - q * HALF


def gather(odd, parts, ext):
    outer, inner, far_outer, far_inner = parts
    for blk, src in ((0, far_outer), (1, outer), (2, inner), (3, far_inner)):
        ext[blk + odd * (3 - 2 * blk)] = src[...]


def cut(info, pos, ext, store):
    top, q, shift = place(info, pos)
    lane = lax.broadcasted_iota(jnp.int32, (RC, HALF), 1)
    back = jnp.where(shift == 0, 0, HALF - shift)
    keep = lane < HALF - shift
    for c in range(2):
        for r in range(0, FULL, RC):
            rot = [pltpu.roll(ext[q + b, c, pl.ds(top + r, RC), :], back, axis=1) for b in range(3)]
            store(c, pl.ds(r, RC), pl.ds(0, HALF), jnp.where(keep, rot[0], rot[1]))
            store(c, pl.ds(r, RC), pl.ds(HALF, HALF), jnp.where(keep, rot[1], rot[2]))


def halve(whole, outer, inner, sem):
    odd = lax.axis_index("tile") % 2
    copies = []
    for k, (side, half) in enumerate(((odd, outer), (1 - odd, inner))):
        lanes = pl.ds(pl.multiple_of(side * HALF, HALF), HALF)
        copies.append(pltpu.make_async_copy(whole.at[0, :, :, lanes], half, sem.at[k]))
        copies[-1].start()
    for copy in copies:
        copy.wait()


def early(info, own_o, own_i, own_on, own_in, prb_hbm, prb1, meas_hbm, kh_hbm, kl_hbm, sort_hbm,
          wown, psi, mp, kh, kl, prb0, ext, lh, rh, mo, fld, cols, meas, sort, sem):
    d = lax.axis_index("depth")
    moves = [(kh_hbm, kh), (kl_hbm, kl), (prb_hbm.at[0], prb0), (meas_hbm, meas), (sort_hbm, sort)]
    copies = [pltpu.make_async_copy(src, dst, sem.at[k]) for k, (src, dst) in enumerate(moves)]
    for copy in copies:
        copy.start()
    gather(lax.axis_index("tile") % 2, (own_o, own_i, own_on, own_in), ext)
    for copy in copies:
        copy.wait()
    probes = (prb0, prb1)

    def position(pos, carry):
        def store(c, rows, at, value):
            wown[pos, c, rows, at] = value

        cut(info, pos, ext, store)
        for c in range(2):
            cols[c] = meas[pos, :, pl.ds(c * HALF, HALF)]
        for par in range(2):
            m = jnp.concatenate([cols[c, pl.ds(par, HALF, stride=2), :] for c in range(2)], axis=1)
            m1 = m.astype(BF16)
            rest = m - m1.astype(F32)
            m2 = rest.astype(BF16)
            m3 = (rest - m2.astype(F32)).astype(BF16)
            mp[pos, par] = dot(m1, sort[...]) + (dot(m2, sort[...]) + dot(m3, sort[...]))

        @pl.when(d == 0)
        def _():
            for mode in range(2):
                for r in range(0, FULL, RC):
                    rr = pl.ds(r, RC)
                    pr, pi = probes[mode][0, rr], probes[mode][1, rr]
                    wr, wi = wown[pos, 0, rr], wown[pos, 1, rr]
                    halves_to_lh(lh, mode, r, pr * wr - pi * wi, pr * wi + pi * wr)
            right(lh, mo, kh, kl, MS, MT)
            prop_middle(mo, rh)
            left(rh, fld, kh, kl, CS, CT)
            for mode in range(2):
                for r in range(0, FULL, RC):
                    pr, pi = natural(fld, mode, r)
                    psi[pos, mode, 0, pl.ds(r, RC)] = pr
                    psi[pos, mode, 1, pl.ds(r, RC)] = pi

        return carry

    lax.fori_loop(0, 2, position, 0)


def grad(info, oth_o, oth_i, oth_on, oth_in, wown, psi0, mp, prb0, prb1, kh, kl, g_o, g_i, g_on, g_in,
         ext, acc, win, psi, lh, rh, mo, fld):
    d = lax.axis_index("depth")
    odd = lax.axis_index("tile") % 2
    gather(odd, (oth_o, oth_i, oth_on, oth_in), ext)
    acc[...] = jnp.zeros(acc.shape, F32)
    probes = (prb0, prb1)

    def position(pos, carry):
        def store(c, rows, at, value):
            win[c, rows, at] = value

        cut(info, pos, ext, store)

        @pl.when(d == 0)
        def _():
            for mode in range(2):
                for r in range(0, FULL, RC):
                    rr = pl.ds(r, RC)
                    pr, pi = psi0[pos, mode, 0, rr], psi0[pos, mode, 1, rr]
                    wr, wi = win[0, rr], win[1, rr]
                    halves_to_lh(lh, mode, r, pr * wr - pi * wi, pr * wi + pi * wr)

        @pl.when(d != 0)
        def _():
            for mode in range(2):
                for r in range(0, FULL, RC):
                    rr = pl.ds(r, RC)
                    pr, pi = probes[mode][0, rr], probes[mode][1, rr]
                    wr, wi = win[0, rr], win[1, rr]
                    halves_to_lh(lh, mode, r, pr * wr - pi * wi, pr * wi + pi * wr)
            right(lh, mo, kh, kl, MS, MT)
            prop_middle(mo, rh)
            left(rh, fld, kh, kl, CS, CT)
            for mode in range(2):
                for r in range(0, FULL, RC):
                    rr = pl.ds(r, RC)
                    pr, pi = natural(fld, mode, r)
                    psi[mode, 0, rr] = pr
                    psi[mode, 1, rr] = pi
                    wr, wi = wown[pos, 0, rr], wown[pos, 1, rr]
                    halves_to_lh(lh, mode, r, pr * wr - pi * wi, pr * wi + pi * wr)

        right(lh, mo, kh, kl, FS, FT)
        for mode in range(2):
            for r in range(0, HALF, RC):
                tp, bt = pl.ds(r, RC), pl.ds(HALF + r, RC)
                for c in range(2):
                    et, eb = mo[c, mode, tp], mo[c, mode, bt]
                    s, t = et + eb, et - eb
                    at = pl.ds(c * HALF, HALF)
                    put(rh, 0, mode, tp, at, s[:, :HALF])
                    put(rh, 0, mode, bt, at, s[:, HALF:])
                    put(rh, 1, mode, tp, at, t[:, :HALF])
                    put(rh, 1, mode, bt, at, t[:, HALF:])
        left(rh, fld, kh, kl, GS, GT)
        for par in range(2):
            for r in range(0, HALF, RC):
                tp, bt = pl.ds(r, RC), pl.ds(HALF + r, RC)
                fr = [fld[par, mode, tp] for mode in range(2)]
                fi = [fld[par, mode, bt] for mode in range(2)]
                resid = (fr[0] * fr[0] + fi[0] * fi[0]) + (fr[1] * fr[1] + fi[1] * fi[1]) - mp[pos, par, tp]
                for mode in range(2):
                    put(rh, par, mode, tp, slice(None), resid * fr[mode])
                    put(rh, par, mode, bt, slice(None), resid * fi[mode])
        left(rh, fld, kh, kl, FS, FT)
        for mode in range(2):
            for r in range(0, FULL, RC):
                rr = pl.ds(r, RC)
                xr, xi = natural(fld, mode, r)
                put(lh, 0, mode, rr, pl.ds(0, HALF), xr[:, :HALF])
                put(lh, 0, mode, rr, pl.ds(HALF, HALF), xi[:, :HALF])
                put(lh, 1, mode, rr, pl.ds(0, HALF), xr[:, HALF:])
                put(lh, 1, mode, rr, pl.ds(HALF, HALF), xi[:, HALF:])
        right(lh, mo, kh, kl, GS, GT)

        def wave_back(mode, rr):
            p, q = mo[0, mode, rr], mo[1, mode, rr]
            y0, y1 = p + q, p - q
            qr = jnp.concatenate([y0[:, :HALF], y1[:, :HALF]], axis=1)
            qi = jnp.concatenate([y0[:, HALF:], y1[:, HALF:]], axis=1)
            return qr, qi

        @pl.when(d == 0)
        def _():
            for mode in range(2):
                for r in range(0, FULL, RC):
                    rr = pl.ds(r, RC)
                    qr, qi = wave_back(mode, rr)
                    wr, wi = win[0, rr], win[1, rr]
                    halves_to_lh(lh, mode, r, wr * qr + wi * qi, wr * qi - wi * qr)
            right(lh, mo, kh, kl, CS, CT)
            prop_middle(mo, rh)
            left(rh, fld, kh, kl, MS, MT)
            for r in range(0, FULL, RC):
                rr = pl.ds(r, RC)
                vr = vi = None
                for mode in range(2):
                    qr, qi = natural(fld, mode, r)
                    pr, pi = probes[mode][0, rr], probes[mode][1, rr]
                    ar, ai = pr * qr + pi * qi, pr * qi - pi * qr
                    vr, vi = (ar, ai) if vr is None else (vr + ar, vi + ai)
                win[0, rr] = vr
                win[1, rr] = vi

        @pl.when(d != 0)
        def _():
            for r in range(0, FULL, RC):
                rr = pl.ds(r, RC)
                vr = vi = None
                for mode in range(2):
                    qr, qi = wave_back(mode, rr)
                    pr, pi = psi[mode, 0, rr], psi[mode, 1, rr]
                    ar, ai = pr * qr + pi * qi, pr * qi - pi * qr
                    vr, vi = (ar, ai) if vr is None else (vr + ar, vi + ai)
                win[0, rr] = vr
                win[1, rr] = vi

        top, q, shift = place(info, pos)
        lane = lax.broadcasted_iota(jnp.int32, (RC, HALF), 1)
        fwd = jnp.where(shift == HALF, 0, shift)
        later = lane >= shift
        zero = jnp.zeros((RC, HALF), F32)
        for c in range(2):
            for r in range(0, FULL, RC):
                rr = pl.ds(r, RC)
                r0 = pltpu.roll(win[c, rr, pl.ds(0, HALF)], fwd, axis=1)
                r1 = pltpu.roll(win[c, rr, pl.ds(HALF, HALF)], fwd, axis=1)
                vals = (jnp.where(later, r0, zero), jnp.where(later, r1, r0), jnp.where(later, zero, r1))
                for b in range(3):
                    acc[q + b, c, pl.ds(top + r, RC), :] = acc[q + b, c, pl.ds(top + r, RC), :] + vals[b]
        return carry

    lax.fori_loop(0, 2, position, 0)
    for blk, out in ((0, g_on), (1, g_o), (2, g_i), (3, g_in)):
        out[...] = acc[blk + odd * (3 - 2 * blk)]


def merge(a, b, ra, rb, out, buf, sem):
    odd = lax.axis_index("tile") % 2
    copies = []
    for c in range(2):
        buf[c, :, pl.ds(pl.multiple_of(odd * HALF, HALF), HALF)] = a[c] + ra[c]
        buf[c, :, pl.ds(pl.multiple_of((1 - odd) * HALF, HALF), HALF)] = b[c] + rb[c]
        copies.append(pltpu.make_async_copy(buf.at[c], out.at[0, c], sem.at[c]))
        copies[-1].start()
    for copy in copies:
        copy.wait()


def step(probe, object_slices, positions, measured):
    tiles = lax.axis_size("tile")
    cross = [(0, 3), (3, 0), (1, 2), (2, 1)]
    pair = [(i, i ^ 1) for i in range(tiles)]
    side = [(i, i + 1) for i in range(1, tiles - 1, 2)]
    side = side + [(j, i) for i, j in side]
    smem = pl.BlockSpec(memory_space=pltpu.SMEM)
    vmem = pl.BlockSpec(memory_space=pltpu.VMEM)
    anyw = pl.BlockSpec(memory_space=pltpu.HBM)
    block = pltpu.VMEM((2, ROWS, HALF), F32)
    own_o, own_i = pl.pallas_call(
        halve,
        out_shape=(block, block),
        in_specs=[anyw],
        out_specs=(vmem, vmem),
        scratch_shapes=[pltpu.SemaphoreType.DMA((2,))],
        name="halve",
        compiler_params=pltpu.CompilerParams(vmem_limit_bytes=2**20),
    )(in_hbm(object_slices))
    oth_o = lax.ppermute(own_o, ("depth", "mode"), cross)
    oth_i = lax.ppermute(own_i, ("depth", "mode"), cross)
    own_on = lax.ppermute(own_o, "tile", side)
    own_in = lax.ppermute(own_i, "tile", pair)
    prb = lax.ppermute(probe, "mode", [(0, 1), (1, 0)])
    oth_on = lax.ppermute(oth_o, "tile", side)
    oth_in = lax.ppermute(oth_i, "tile", pair)
    info = positions
    high, low, sort = (jnp.asarray(x) for x in tables())
    p1 = in_vmem(prb[0])
    wown, psi, mp, kh, kl, p0 = pl.pallas_call(
        early,
        out_shape=(pltpu.VMEM((2, 2, FULL, FULL), F32), pltpu.VMEM((2, 2, 2, FULL, FULL), F32),
                   pltpu.VMEM((2, 2, HALF, FULL), F32), pltpu.VMEM(high.shape, BF16),
                   pltpu.VMEM(low.shape, BF16), pltpu.VMEM((2, FULL, FULL), F32)),
        in_specs=[smem] + [vmem] * 4 + [anyw, vmem] + [anyw] * 4,
        out_specs=(vmem,) * 6,
        scratch_shapes=[
            pltpu.VMEM((4, 2, ROWS, HALF), F32),
            pltpu.VMEM((2, 2, 2, FULL, FULL), BF16),
            pltpu.VMEM((2, 2, 2, FULL, FULL), BF16),
            pltpu.VMEM((2, 2, FULL, FULL), F32),
            pltpu.VMEM((2, 2, FULL, FULL), F32),
            pltpu.VMEM((2, FULL, HALF), F32),
            pltpu.VMEM((2, FULL, FULL), F32),
            pltpu.VMEM((FULL, FULL), BF16),
            pltpu.SemaphoreType.DMA((5,)),
        ],
        name="early",
        compiler_params=pltpu.CompilerParams(vmem_limit_bytes=LIMIT),
    )(info, *map(in_vmem, (own_o, own_i, own_on, own_in)), in_hbm(probe), p1, *map(in_hbm, (measured, high, low, sort)))
    g_o, g_i, g_on, g_in = pl.pallas_call(
        grad,
        out_shape=(block,) * 4,
        in_specs=[smem] + [vmem] * 11,
        out_specs=(vmem,) * 4,
        scratch_shapes=[
            pltpu.VMEM((4, 2, ROWS, HALF), F32),
            pltpu.VMEM((4, 2, ROWS, HALF), F32),
            pltpu.VMEM((2, FULL, FULL), F32),
            pltpu.VMEM((2, 2, FULL, FULL), F32),
            pltpu.VMEM((2, 2, 2, FULL, FULL), BF16),
            pltpu.VMEM((2, 2, 2, FULL, FULL), BF16),
            pltpu.VMEM((2, 2, FULL, FULL), F32),
            pltpu.VMEM((2, 2, FULL, FULL), F32),
        ],
        name="grad",
        compiler_params=pltpu.CompilerParams(vmem_limit_bytes=LIMIT),
    )(info, *map(in_vmem, (oth_o, oth_i, oth_on, oth_in, wown, psi, mp, p0)), p1, in_vmem(kh), in_vmem(kl))
    r_o = lax.ppermute(g_on, "tile", side)
    r_i = lax.ppermute(g_in, "tile", pair)
    return pl.pallas_call(
        merge,
        out_shape=jax.ShapeDtypeStruct((1, 2, ROWS, FULL), F32),
        in_specs=[vmem] * 4,
        out_specs=anyw,
        scratch_shapes=[pltpu.VMEM((2, ROWS, FULL), F32), pltpu.SemaphoreType.DMA((2,))],
        name="merge",
        compiler_params=pltpu.CompilerParams(vmem_limit_bytes=LIMIT),
    )(*map(in_vmem, (g_o, g_i, r_o, r_i)))


def in_hbm(x):
    return pltpu.with_memory_space_constraint(x, pltpu.HBM)


def in_vmem(x):
    return pltpu.with_memory_space_constraint(x, pltpu.VMEM)


def solution(mesh):
    placed = (
        P("mode", None, None, None),
        P("depth", None, None, "tile"),
        P("tile", None),
        P("tile", None, None),
    )
    return jax.shard_map(
        step, mesh=mesh, in_specs=placed, out_specs=P("depth", None, None, "tile"), check_vma=False
    )
```

time: 65.3 us -> 52.1 us (0.80)
  waiting for transfers between devices: 29.8 us -> 19.1 us
  other arithmetic: 1.86 us -> 0 us
  local copies, waits for them, and re-layouts: 1.66 us -> 0.67 us
    ppermute x9, waiting for transfers between devices: 29.8 us -> 19.1 us  [the longest x1 7.73 us: step(): r_o = lax.ppermute(g_on, 'tile', side)]
    select_n x1 -> x0, other arithmetic: 1.23 us -> none  [body(): own_i = jnp.where(odd == 0, rgt, lft)]
    unnamed x22 -> x2, local copies, waits for them, and re-layouts: 1.58 us -> 0.67 us
    pallas_call x2 -> x4, Pallas kernels: 17.2 us -> 17.5 us  [the longest x1 9.7 us: step(): pl.pallas_call(grad, out_shape=(block,) * 4, in_specs=[smem] + [vmem] * 1...]
  transfers between devices with their start and end apart: 9 -> 9, of which waited for: 4 -> 3; matrix products, arithmetic and copies ran while one was open for 1% -> 0% of each run, Pallas kernels for 0% -> 11%
where the time goes in v1:
time: 52.1 us; the launch traced here: 51.3 us
  waiting for transfers between devices  19.1 us (37%)
  Pallas kernels  17.5 us (34%)
  starting transfers between devices  13.9 us (27%)
  local copies, waits for them, and re-layouts  0.67 us (1%)
    pallas_call x1, Pallas kernels, step(): pl.pallas_call(grad, out_shape=(block,) * 4, in_specs=[smem] + [vmem] * 1...  9.7 us
    ppermute x1, waiting for transfers between devices, step(): r_o = lax.ppermute(g_on, 'tile', side)  7.73 us
    ppermute x1, waiting for transfers between devices, step(): oth_o = lax.ppermute(own_o, ('depth', 'mode'), cross)  5.99 us
    pallas_call x1, Pallas kernels, step(): pl.pallas_call(early, out_shape=(pltpu.VMEM((2, 2, FULL, FULL), F32), plt...  5.71 us
    ppermute x1, waiting for transfers between devices, step(): oth_i = lax.ppermute(own_i, ('depth', 'mode'), cross)  5.38 us
    ppermute x1, starting transfers between devices, step(): r_o = lax.ppermute(g_on, 'tile', side)  4.57 us
    ppermute x1, starting transfers between devices, step(): own_on = lax.ppermute(own_o, 'tile', side)  3.06 us
    ppermute x1, starting transfers between devices, step(): oth_o = lax.ppermute(own_o, ('depth', 'mode'), cross)  2.85 us
  transfers between devices with their start and end apart: 9, of which 3 were waited for; matrix products, arithmetic and copies ran while one was open for 0% of the time, Pallas kernels for 11%

profile of v1, /device:TPU:128, one launch (start us, length us, event | category | flops | bytes accessed | tf_op | source)
XLA Modules:
  0.0 51.3 jit_solution(9677490194762337845)
XLA Ops:
  0.0 1.1 %halve.1 = (f32[2,384,128]{2,1,0:T(8,128)S(1)}, f32[2,384,128]{2,1,0:T(8,128)S(1)}) custom-call(f32[1,2,384,256]{3,2,1,0:T(8,128)} %whole.1), custom_call_target="tpu_custom_call" | custom-call | tf_op jit(solution)/shard_map/halve/pallas_call | solution.py:359
  1.1 2.8 %collective-permute-start = (f32[2,384,128]{2,1,0:T(8,128)S(1)}, f32[2,384,128]{2,1,0:T(8,128)S(1)}, u32[]{:S(2)}, u32[]{:S(2)}) collective-permute-start(f32[2,384,128]{2,1,0:T(8,128)S(1)} %get-tuple-element.17.own_o), channel_id=1, source_target_pairs={{0,192},{192,0},{64,128},{128,64},{1,193},{193,1},{65,129},{129,65... | collective-permute-start | bytes 1179656 | tf_op jit(solution)/shard_map/ppermute | solution.py:368
  4.0 0.5 collective-permute-start.1
  4.5 0.3 collective-permute-start.6
  4.7 3.1 %collective-permute-start.4 = (f32[2,384,128]{2,1,0:T(8,128)S(1)}, f32[2,384,128]{2,1,0:T(8,128)S(1)}, u32[]{:S(2)}, u32[]{:S(2)}) collective-permute-start(f32[2,384,128]{2,1,0:T(8,128)S(1)} %get-tuple-element.17.own_o), channel_id=1, source_target_pairs={{1,2},{3,4},{5,6},{7,8},{9,10},{11,12},{13,14},{15,16},{17,18},{19... | collective-permute-start | bytes 1179656 | tf_op jit(solution)/shard_map/ppermute | solution.py:370
  7.8 0.6 %collective-permute-start.5 = (f32[2,384,128]{2,1,0:T(8,128)S(1)}, f32[2,384,128]{2,1,0:T(8,128)S(1)}, u32[]{:S(2)}, u32[]{:S(2)}) collective-permute-start(f32[2,384,128]{2,1,0:T(8,128)S(1)} %get-tuple-element.18.own_i), channel_id=1, source_target_pairs={{0,1},{1,0},{2,3},{3,2},{4,5},{5,4},{6,7},{7,6},{8,9},{9,8},{10,11... | collective-permute-start | bytes 1179656 | tf_op jit(solution)/shard_map/ppermute | solution.py:371
  8.4 6.0 %collective-permute-done.oth_o = f32[2,384,128]{2,1,0:T(8,128)S(1)} collective-permute-done((f32[2,384,128]{2,1,0:T(8,128)S(1)}, f32[2,384,128]{2,1,0:T(8,128)S(1)}, u32[]{:S(2)}, u32[]{:S(2)}) %collective-permute-start) | collective-permute-done | bytes 393248 | tf_op jit(solution)/shard_map/ppermute | solution.py:368
  14.4 1.9 %collective-permute-start.2 = (f32[2,384,128]{2,1,0:T(8,128)S(1)}, f32[2,384,128]{2,1,0:T(8,128)S(1)}, u32[]{:S(2)}, u32[]{:S(2)}) collective-permute-start(f32[2,384,128]{2,1,0:T(8,128)S(1)} %collective-permute-done.oth_o), channel_id=1, source_target_pairs={{1,2},{3,4},{5,6},{7,8},{9,10},{11,12},{13,14},{15,16},{17,18},{19... | collective-permute-start | bytes 1179656 | tf_op jit(solution)/shard_map/ppermute | solution.py:373
  16.3 5.4 %collective-permute-done.1.oth_i = f32[2,384,128]{2,1,0:T(8,128)S(1)} collective-permute-done((f32[2,384,128]{2,1,0:T(8,128)S(1)}, f32[2,384,128]{2,1,0:T(8,128)S(1)}, u32[]{:S(2)}, u32[]{:S(2)}) %collective-permute-start.1) | collective-permute-done | bytes 393248 | tf_op jit(solution)/shard_map/ppermute | solution.py:369
  21.7 0.0 collective-permute-start.3
  21.7 0.0 collective-permute-done.4.own_on
  21.7 0.0 collective-permute-done.5.own_in
  21.7 0.0 collective-permute-done.6
  21.7 0.0 copy-start
  21.8 0.7 %copy-done = s32[2,2]{1,0:T(2,128)S(1)} copy-done((s32[2,2]{1,0:T(2,128)S(1)}, s32[2,2]{1,0:T(2,128)}, u32[]{:S(2)}) %copy-start) | copy-done | bytes 40
  22.4 5.7 %early.1 = (f32[2,2,256,256]{3,2,1,0:T(8,128)S(1)}, f32[2,2,2,256,256]{4,3,2,1,0:T(8,128)S(1)}, f32[2,2,128,256]{3,2,1,0:T(8,128)S(1)}, bf16[8,256,256]{2,1,0:T(...) custom-call(s32[2,2]{1,0:T(2,128)S(1)} %copy-done, ...), custom_call_target="tpu_custom_call" | custom-call | tf_op jit(solution)/shard_map/early/pallas_call | solution.py:378
  28.1 0.0 collective-permute-done.2.oth_on
  28.2 0.0 collective-permute-done.3.oth_in
  28.2 9.7 %grad.1 = (f32[2,384,128]{2,1,0:T(8,128)S(1)}, f32[2,384,128]{2,1,0:T(8,128)S(1)}, f32[2,384,128]{2,1,0:T(8,128)S(1)}, f32[2,384,128]{2,1,0:T(8,128)S(1)}) custom-call(s32[2,2]{1,0:T(2,128)S(1)} %copy-done, f32[2,384,128]{2,1,0:T(8,128)S(1)} %collective-permute-done.oth_o, f32[2,384,128]{2,1,0:T(8,128)S(1)} %collective-permute-done.1.oth_i, ...), custom_call_target="tpu_custom_call" | custom-call | tf_op jit(solution)/shard_map/grad/pallas_call | solution.py:399
  37.9 4.6 %collective-permute-start.7 = (f32[2,384,128]{2,1,0:T(8,128)S(1)}, f32[2,384,128]{2,1,0:T(8,128)S(1)}, u32[]{:S(2)}, u32[]{:S(2)}) collective-permute-start(f32[2,384,128]{2,1,0:T(8,128)S(1)} %get-tuple-element.27), channel_id=1, source_target_pairs={{1,2},{3,4},{5,6},{7,8},{9,10},{11,12},{13,14},{15,16},{17,18},{19... | collective-permute-start | bytes 1179656 | tf_op jit(solution)/shard_map/ppermute | solution.py:417
  42.5 0.1 collective-permute-start.8
  42.6 7.7 %collective-permute-done.7.ra = f32[2,384,128]{2,1,0:T(8,128)S(1)} collective-permute-done((f32[2,384,128]{2,1,0:T(8,128)S(1)}, f32[2,384,128]{2,1,0:T(8,128)S(1)}, u32[]{:S(2)}, u32[]{:S(2)}) %collective-permute-start.7) | collective-permute-done | bytes 393248 | tf_op jit(solution)/shard_map/ppermute | solution.py:417
  50.3 0.0 collective-permute-done.8.rb
  50.3 1.0 %merge.1 = f32[1,2,384,256]{3,2,1,0:T(8,128)} custom-call(f32[2,384,128]{2,1,0:T(8,128)S(1)} %get-tuple-element.25.a, f32[2,384,128]{2,1,0:T(8,128)S(1)} %get-tuple-element.26.b, f32[2,384,128]{2,1,0:T(8,128)S(1)} %collective-permute-done.7.ra, f32[2,384,128]{2,1,0:T(8,128)S(1)} %collective-permute-done.8.rb), custom_call_target="tpu_custom_call" | custom-call | tf_op jit(solution)/shard_map/merge/pallas_call | solution.py:419
Async XLA Ops:
  1.1 13.3 %collective-permute-start = (f32[2,384,128]{2,1,0:T(8,128)S(1)}, f32[2,384,128]{2,1,0:T(8,128)S(1)}, u32[]{:S(2)}, u32[]{:S(2)}) collective-permute-start(f32[2,384,128]{2,1,0:T(8,128)S(1)} %get-tuple-element.17.own_o), channel_id=1, source_target_pairs={{0,192},{192,0},{64,128},{128,64},{1,193},{193,1},{65,129},{129,65... | collective-permute-start | bytes 1179656 | tf_op jit(solution)/shard_map/ppermute | solution.py:368
  4.0 17.7 %collective-permute-start.1 = (f32[2,384,128]{2,1,0:T(8,128)S(1)}, f32[2,384,128]{2,1,0:T(8,128)S(1)}, u32[]{:S(2)}, u32[]{:S(2)}) collective-permute-start(f32[2,384,128]{2,1,0:T(8,128)S(1)} %get-tuple-element.18.own_i), channel_id=1, source_target_pairs={{0,192},{192,0},{64,128},{128,64},{1,193},{193,1},{65,129},{129,65... | collective-permute-start | bytes 1179656 | tf_op jit(solution)/shard_map/ppermute | solution.py:369
  4.5 17.3 %collective-permute-start.6 = (f32[1,2,256,256]{3,2,1,0:T(8,128)}, f32[1,2,256,256]{3,2,1,0:T(8,128)S(1)}, u32[]{:S(2)}, u32[]{:S(2)}) collective-permute-start(f32[1,2,256,256]{3,2,1,0:T(8,128)} %prb_hbm.1), channel_id=1, source_target_pairs={{0,64},{64,0},{1,65},{65,1},{2,66},{66,2},{3,67},{67,3},{4,68},{68... | collective-permute-start | bytes 1572872 | tf_op jit(solution)/shard_map/ppermute | solution.py:372
  4.7 17.0 %collective-permute-start.4 = (f32[2,384,128]{2,1,0:T(8,128)S(1)}, f32[2,384,128]{2,1,0:T(8,128)S(1)}, u32[]{:S(2)}, u32[]{:S(2)}) collective-permute-start(f32[2,384,128]{2,1,0:T(8,128)S(1)} %get-tuple-element.17.own_o), channel_id=1, source_target_pairs={{1,2},{3,4},{5,6},{7,8},{9,10},{11,12},{13,14},{15,16},{17,18},{19... | collective-permute-start | bytes 1179656 | tf_op jit(solution)/shard_map/ppermute | solution.py:370
  7.8 13.9 %collective-permute-start.5 = (f32[2,384,128]{2,1,0:T(8,128)S(1)}, f32[2,384,128]{2,1,0:T(8,128)S(1)}, u32[]{:S(2)}, u32[]{:S(2)}) collective-permute-start(f32[2,384,128]{2,1,0:T(8,128)S(1)} %get-tuple-element.18.own_i), channel_id=1, source_target_pairs={{0,1},{1,0},{2,3},{3,2},{4,5},{5,4},{6,7},{7,6},{8,9},{9,8},{10,11... | collective-permute-start | bytes 1179656 | tf_op jit(solution)/shard_map/ppermute | solution.py:371
  14.4 13.7 %collective-permute-start.2 = (f32[2,384,128]{2,1,0:T(8,128)S(1)}, f32[2,384,128]{2,1,0:T(8,128)S(1)}, u32[]{:S(2)}, u32[]{:S(2)}) collective-permute-start(f32[2,384,128]{2,1,0:T(8,128)S(1)} %collective-permute-done.oth_o), channel_id=1, source_target_pairs={{1,2},{3,4},{5,6},{7,8},{9,10},{11,12},{13,14},{15,16},{17,18},{19... | collective-permute-start | bytes 1179656 | tf_op jit(solution)/shard_map/ppermute | solution.py:373
  21.7 6.4 %collective-permute-start.3 = (f32[2,384,128]{2,1,0:T(8,128)S(1)}, f32[2,384,128]{2,1,0:T(8,128)S(1)}, u32[]{:S(2)}, u32[]{:S(2)}) collective-permute-start(f32[2,384,128]{2,1,0:T(8,128)S(1)} %collective-permute-done.1.oth_i), channel_id=1, source_target_pairs={{0,1},{1,0},{2,3},{3,2},{4,5},{5,4},{6,7},{7,6},{8,9},{9,8},{10,11... | collective-permute-start | bytes 1179656 | tf_op jit(solution)/shard_map/ppermute | solution.py:374
  21.7 0.7 %copy-start = (s32[2,2]{1,0:T(2,128)S(1)}, s32[2,2]{1,0:T(2,128)}, u32[]{:S(2)}) copy-start(s32[2,2]{1,0:T(2,128)} %info.3) | copy-start | bytes 52
  37.9 12.4 %collective-permute-start.7 = (f32[2,384,128]{2,1,0:T(8,128)S(1)}, f32[2,384,128]{2,1,0:T(8,128)S(1)}, u32[]{:S(2)}, u32[]{:S(2)}) collective-permute-start(f32[2,384,128]{2,1,0:T(8,128)S(1)} %get-tuple-element.27), channel_id=1, source_target_pairs={{1,2},{3,4},{5,6},{7,8},{9,10},{11,12},{13,14},{15,16},{17,18},{19... | collective-permute-start | bytes 1179656 | tf_op jit(solution)/shard_map/ppermute | solution.py:417
  42.5 7.8 %collective-permute-start.8 = (f32[2,384,128]{2,1,0:T(8,128)S(1)}, f32[2,384,128]{2,1,0:T(8,128)S(1)}, u32[]{:S(2)}, u32[]{:S(2)}) collective-permute-start(f32[2,384,128]{2,1,0:T(8,128)S(1)} %get-tuple-element.28), channel_id=1, source_target_pairs={{0,1},{1,0},{2,3},{3,2},{4,5},{5,4},{6,7},{7,6},{8,9},{9,8},{10,11... | collective-permute-start | bytes 1179656 | tf_op jit(solution)/shard_map/ppermute | solution.py:418

commit v2 on v1

--- a/solution.py
+++ b/solution.py
@@ -147,23 +147,17 @@
         copy.wait()
 
 
-def early(info, own_o, own_i, own_on, own_in, prb_hbm, prb1, meas_hbm, kh_hbm, kl_hbm, sort_hbm,
-          wown, psi, mp, kh, kl, prb0, ext, lh, rh, mo, fld, cols, meas, sort, sem):
-    d = lax.axis_index("depth")
-    moves = [(kh_hbm, kh), (kl_hbm, kl), (prb_hbm.at[0], prb0), (meas_hbm, meas), (sort_hbm, sort)]
+def prepare(where, prb_hbm, meas_hbm, kh_hbm, kl_hbm, sort_hbm, info, mp, kh, kl, prb0, cols, meas, sort, sem):
+    moves = [(meas_hbm, meas), (sort_hbm, sort), (kh_hbm, kh), (kl_hbm, kl), (prb_hbm.at[0], prb0)]
     copies = [pltpu.make_async_copy(src, dst, sem.at[k]) for k, (src, dst) in enumerate(moves)]
     for copy in copies:
         copy.start()
-    gather(lax.axis_index("tile") % 2, (own_o, own_i, own_on, own_in), ext)
-    for copy in copies:
+    for pos in range(2):
+        for k in range(2):
+            info[pos, k] = where[pos, k]
+    for copy in copies[:2]:
         copy.wait()
-    probes = (prb0, prb1)
-
-    def position(pos, carry):
-        def store(c, rows, at, value):
-            wown[pos, c, rows, at] = value
-
-        cut(info, pos, ext, store)
+    for pos in range(2):
         for c in range(2):
             cols[c] = meas[pos, :, pl.ds(c * HALF, HALF)]
         for par in range(2):
@@ -173,6 +167,20 @@
             m2 = rest.astype(BF16)
             m3 = (rest - m2.astype(F32)).astype(BF16)
             mp[pos, par] = dot(m1, sort[...]) + (dot(m2, sort[...]) + dot(m3, sort[...]))
+    for copy in copies[2:]:
+        copy.wait()
+
+
+def early(info, own_o, own_i, own_on, own_in, prb0, prb1, kh, kl, wown, psi, ext, lh, rh, mo, fld):
+    d = lax.axis_index("depth")
+    gather(lax.axis_index("tile") % 2, (own_o, own_i, own_on, own_in), ext)
+    probes = (prb0, prb1)
+
+    def position(pos, carry):
+        def store(c, rows, at, value):
+            wown[pos, c, rows, at] = value
+
+        cut(info, pos, ext, store)
 
         @pl.when(d == 0)
         def _():
@@ -338,7 +346,7 @@
     odd = lax.axis_index("tile") % 2
     copies = []
     for c in range(2):
-        buf[c, :, pl.ds(pl.multiple_of(odd * HALF, HALF), HALF)] = a[c] + ra[c]
+        buf[c, :, pl.ds(pl.multiple_of(odd * HALF, HALF), HALF)] = a[c] + ra[odd, c]
         buf[c, :, pl.ds(pl.multiple_of((1 - odd) * HALF, HALF), HALF)] = b[c] + rb[c]
         copies.append(pltpu.make_async_copy(buf.at[c], out.at[0, c], sem.at[c]))
         copies[-1].start()
@@ -372,30 +380,36 @@
     prb = lax.ppermute(probe, "mode", [(0, 1), (1, 0)])
     oth_on = lax.ppermute(oth_o, "tile", side)
     oth_in = lax.ppermute(oth_i, "tile", pair)
-    info = positions
     high, low, sort = (jnp.asarray(x) for x in tables())
-    p1 = in_vmem(prb[0])
-    wown, psi, mp, kh, kl, p0 = pl.pallas_call(
-        early,
-        out_shape=(pltpu.VMEM((2, 2, FULL, FULL), F32), pltpu.VMEM((2, 2, 2, FULL, FULL), F32),
-                   pltpu.VMEM((2, 2, HALF, FULL), F32), pltpu.VMEM(high.shape, BF16),
+    limit = pltpu.CompilerParams(vmem_limit_bytes=LIMIT)
+    pair_of = pltpu.VMEM((2, 2, FULL, FULL), F32)
+    info, mp, kh, kl, p0 = pl.pallas_call(
+        prepare,
+        out_shape=(pltpu.SMEM((2, 2), jnp.int32), pltpu.VMEM((2, 2, HALF, FULL), F32), pltpu.VMEM(high.shape, BF16),
                    pltpu.VMEM(low.shape, BF16), pltpu.VMEM((2, FULL, FULL), F32)),
-        in_specs=[smem] + [vmem] * 4 + [anyw, vmem] + [anyw] * 4,
-        out_specs=(vmem,) * 6,
+        in_specs=[smem] + [anyw] * 5,
+        out_specs=(smem,) + (vmem,) * 4,
         scratch_shapes=[
-            pltpu.VMEM((4, 2, ROWS, HALF), F32),
-            pltpu.VMEM((2, 2, 2, FULL, FULL), BF16),
-            pltpu.VMEM((2, 2, 2, FULL, FULL), BF16),
-            pltpu.VMEM((2, 2, FULL, FULL), F32),
-            pltpu.VMEM((2, 2, FULL, FULL), F32),
             pltpu.VMEM((2, FULL, HALF), F32),
             pltpu.VMEM((2, FULL, FULL), F32),
             pltpu.VMEM((FULL, FULL), BF16),
             pltpu.SemaphoreType.DMA((5,)),
         ],
+        name="prepare",
+        compiler_params=limit,
+    )(positions, *map(in_hbm, (probe, measured, high, low, sort)))
+    info = pltpu.with_memory_space_constraint(info, pltpu.SMEM)
+    p0, p1, kh, kl, mp = map(in_vmem, (p0, prb[0], kh, kl, mp))
+    fields = [pltpu.VMEM((2, 2, 2, FULL, FULL), BF16)] * 2 + [pair_of] * 2
+    wown, psi = pl.pallas_call(
+        early,
+        out_shape=(pair_of, pltpu.VMEM((2, 2, 2, FULL, FULL), F32)),
+        in_specs=[smem] + [vmem] * 8,
+        out_specs=(vmem,) * 2,
+        scratch_shapes=[pltpu.VMEM((4, 2, ROWS, HALF), F32)] + fields,
         name="early",
-        compiler_params=pltpu.CompilerParams(vmem_limit_bytes=LIMIT),
-    )(info, *map(in_vmem, (own_o, own_i, own_on, own_in)), in_hbm(probe), p1, *map(in_hbm, (measured, high, low, sort)))
+        compiler_params=limit,
+    )(info, *map(in_vmem, (own_o, own_i, own_on, own_in)), p0, p1, kh, kl)
     g_o, g_i, g_on, g_in = pl.pallas_call(
         grad,
         out_shape=(block,) * 4,
@@ -405,17 +419,15 @@
             pltpu.VMEM((4, 2, ROWS, HALF), F32),
             pltpu.VMEM((4, 2, ROWS, HALF), F32),
             pltpu.VMEM((2, FULL, FULL), F32),
-            pltpu.VMEM((2, 2, FULL, FULL), F32),
-            pltpu.VMEM((2, 2, 2, FULL, FULL), BF16),
-            pltpu.VMEM((2, 2, 2, FULL, FULL), BF16),
-            pltpu.VMEM((2, 2, FULL, FULL), F32),
-            pltpu.VMEM((2, 2, FULL, FULL), F32),
-        ],
+            pair_of,
+        ] + fields,
         name="grad",
-        compiler_params=pltpu.CompilerParams(vmem_limit_bytes=LIMIT),
-    )(info, *map(in_vmem, (oth_o, oth_i, oth_on, oth_in, wown, psi, mp, p0)), p1, in_vmem(kh), in_vmem(kl))
-    r_o = lax.ppermute(g_on, "tile", side)
+        compiler_params=limit,
+    )(info, *map(in_vmem, (oth_o, oth_i, oth_on, oth_in, wown, psi)), mp, p0, p1, kh, kl)
+    groups = [[m * tiles + i, m * tiles + i + 1] for m in range(2) for i in range(1, tiles - 1, 2)]
+    groups = groups + [[i, tiles + i] for i in (0, tiles - 1)]
     r_i = lax.ppermute(g_in, "tile", pair)
+    r_o = lax.all_gather(g_on, ("mode", "tile"), axis_index_groups=groups)
     return pl.pallas_call(
         merge,
         out_shape=jax.ShapeDtypeStruct((1, 2, ROWS, FULL), F32),
@@ -442,6 +454,4 @@
         P("tile", None),
         P("tile", None, None),
     )
-    return jax.shard_map(
-        step, mesh=mesh, in_specs=placed, out_specs=P("depth", None, None, "tile"), check_vma=False
-    )
+    return jax.shard_map(step, mesh=mesh, in_specs=placed, out_specs=P("depth", None, None, "tile"), check_vma=False)

time: 52.1 us -> 50 us (0.960)
  blocking collectives: 0 us -> 11.2 us
  waiting for transfers between devices: 19.1 us -> 11.4 us
  starting transfers between devices: 13.9 us -> 9.78 us
  Pallas kernels: 17.5 us -> 16.5 us
    all_gather x0 -> x1, blocking collectives: none -> 11.2 us  [step(): r_o = lax.all_gather(g_on, ('mode', 'tile'), axis_index_groups=groups)]
    ppermute x1 -> x0, waiting for transfers between devices: 7.73 us -> none  [step(): r_o = lax.ppermute(g_on, 'tile', side)]
    ppermute x1 -> x0, starting transfers between devices: 4.57 us -> none  [step(): r_o = lax.ppermute(g_on, 'tile', side)]
    pallas_call x1, Pallas kernels: 9.7 us -> 8.69 us  [step(): pl.pallas_call(grad, out_shape=(block,) * 4, in_specs=[smem] + [vmem] * 1...]
    pallas_call x1 -> x2, Pallas kernels: 5.71 us -> 5.68 us  [the longest x1 3.22 us: step(): pl.pallas_call(early, out_shape=(pair_of, pltpu.VMEM((2, 2, 2, FULL, FULL...]
  transfers between devices with their start and end apart: 9 -> 8, of which waited for: 3 -> 2; matrix products, arithmetic and copies ran while one was open for 0% -> 0% of each run, Pallas kernels for 11% -> 11%
where the time goes in v2:
time: 50 us; the launch traced here: 49.6 us
  Pallas kernels  16.5 us (33%)
  waiting for transfers between devices  11.4 us (23%)
  blocking collectives  11.2 us (22%)
  starting transfers between devices  9.78 us (20%)
  local copies, waits for them, and re-layouts  0.68 us (1%)
    all_gather x1, blocking collectives, step(): r_o = lax.all_gather(g_on, ('mode', 'tile'), axis_index_groups=groups)  11.2 us
    pallas_call x1, Pallas kernels, step(): pl.pallas_call(grad, out_shape=(block,) * 4, in_specs=[smem] + [vmem] * 1...  8.69 us
    ppermute x1, waiting for transfers between devices, step(): oth_o = lax.ppermute(own_o, ('depth', 'mode'), cross)  5.99 us
    ppermute x1, waiting for transfers between devices, step(): oth_i = lax.ppermute(own_i, ('depth', 'mode'), cross)  5.38 us
    pallas_call x1, Pallas kernels, step(): pl.pallas_call(early, out_shape=(pair_of, pltpu.VMEM((2, 2, 2, FULL, FULL...  3.22 us
    ppermute x1, starting transfers between devices, step(): own_on = lax.ppermute(own_o, 'tile', side)  3.06 us
    ppermute x1, starting transfers between devices, step(): oth_o = lax.ppermute(own_o, ('depth', 'mode'), cross)  2.85 us
    pallas_call x1, Pallas kernels, step(): pl.pallas_call(prepare, out_shape=(pltpu.SMEM((2, 2), jnp.int32), pltpu.V...  2.46 us
  transfers between devices with their start and end apart: 8, of which 2 were waited for; matrix products, arithmetic and copies ran while one was open for 0% of the time, Pallas kernels for 11%

profile of v2, /device:TPU:128, one launch (start us, length us, event | category | flops | bytes accessed | tf_op | source)
XLA Modules:
  0.0 49.6 jit_solution(2917455130349359532)
XLA Ops:
  0.0 1.1 %halve.1 = (f32[2,384,128]{2,1,0:T(8,128)S(1)}, f32[2,384,128]{2,1,0:T(8,128)S(1)}) custom-call(f32[1,2,384,256]{3,2,1,0:T(8,128)} %whole.1), custom_call_target="tpu_custom_call" | custom-call | tf_op jit(solution)/shard_map/halve/pallas_call | solution.py:367
  1.1 2.8 %collective-permute-start = (f32[2,384,128]{2,1,0:T(8,128)S(1)}, f32[2,384,128]{2,1,0:T(8,128)S(1)}, u32[]{:S(2)}, u32[]{:S(2)}) collective-permute-start(f32[2,384,128]{2,1,0:T(8,128)S(1)} %get-tuple-element.19.own_o), channel_id=1, source_target_pairs={{0,192},{192,0},{64,128},{128,64},{1,193},{193,1},{65,129},{129,65... | collective-permute-start | bytes 1179656 | tf_op jit(solution)/shard_map/ppermute | solution.py:376
  4.0 0.5 collective-permute-start.1
  4.5 0.3 collective-permute-start.6
  4.7 3.1 %collective-permute-start.4 = (f32[2,384,128]{2,1,0:T(8,128)S(1)}, f32[2,384,128]{2,1,0:T(8,128)S(1)}, u32[]{:S(2)}, u32[]{:S(2)}) collective-permute-start(f32[2,384,128]{2,1,0:T(8,128)S(1)} %get-tuple-element.19.own_o), channel_id=1, source_target_pairs={{1,2},{3,4},{5,6},{7,8},{9,10},{11,12},{13,14},{15,16},{17,18},{19... | collective-permute-start | bytes 1179656 | tf_op jit(solution)/shard_map/ppermute | solution.py:378
  7.8 0.6 %collective-permute-start.5 = (f32[2,384,128]{2,1,0:T(8,128)S(1)}, f32[2,384,128]{2,1,0:T(8,128)S(1)}, u32[]{:S(2)}, u32[]{:S(2)}) collective-permute-start(f32[2,384,128]{2,1,0:T(8,128)S(1)} %get-tuple-element.20.own_i), channel_id=1, source_target_pairs={{0,1},{1,0},{2,3},{3,2},{4,5},{5,4},{6,7},{7,6},{8,9},{9,8},{10,11... | collective-permute-start | bytes 1179656 | tf_op jit(solution)/shard_map/ppermute | solution.py:379
  8.4 6.0 %collective-permute-done.oth_o = f32[2,384,128]{2,1,0:T(8,128)S(1)} collective-permute-done((f32[2,384,128]{2,1,0:T(8,128)S(1)}, f32[2,384,128]{2,1,0:T(8,128)S(1)}, u32[]{:S(2)}, u32[]{:S(2)}) %collective-permute-start) | collective-permute-done | bytes 393248 | tf_op jit(solution)/shard_map/ppermute | solution.py:376
  14.4 1.9 %collective-permute-start.2 = (f32[2,384,128]{2,1,0:T(8,128)S(1)}, f32[2,384,128]{2,1,0:T(8,128)S(1)}, u32[]{:S(2)}, u32[]{:S(2)}) collective-permute-start(f32[2,384,128]{2,1,0:T(8,128)S(1)} %collective-permute-done.oth_o), channel_id=1, source_target_pairs={{1,2},{3,4},{5,6},{7,8},{9,10},{11,12},{13,14},{15,16},{17,18},{19... | collective-permute-start | bytes 1179656 | tf_op jit(solution)/shard_map/ppermute | solution.py:381
  16.3 5.4 %collective-permute-done.1.oth_i = f32[2,384,128]{2,1,0:T(8,128)S(1)} collective-permute-done((f32[2,384,128]{2,1,0:T(8,128)S(1)}, f32[2,384,128]{2,1,0:T(8,128)S(1)}, u32[]{:S(2)}, u32[]{:S(2)}) %collective-permute-start.1) | collective-permute-done | bytes 393248 | tf_op jit(solution)/shard_map/ppermute | solution.py:377
  21.7 0.0 collective-permute-start.3
  21.7 0.0 copy-start
  21.7 0.7 %copy-done = s32[2,2]{1,0:T(2,128)S(1)} copy-done((s32[2,2]{1,0:T(2,128)S(1)}, s32[2,2]{1,0:T(2,128)}, u32[]{:S(2)}) %copy-start) | copy-done | bytes 40
  22.4 2.5 %prepare.1 = (s32[2,2]{1,0:T(2,128)S(4)}, f32[2,2,128,256]{3,2,1,0:T(8,128)S(1)}, bf16[8,256,256]{2,1,0:T(8,128)(2,1)S(1)}, bf16[8,256,256]{2,1,0:T(8,128)(2,1)S(1)}, f32[2,256,256]{2,1,0:T(8,128)S(1)}) custom-call(s32[2,2]{1,0:T(2,128)S(1)} %copy-done, f32[1,2,256,256]{3,2,1,0:T(8,128)} %prb_hbm.1, f32[2,256,256]{2,1,0:T(8,128)} %meas_hbm.1, ...), custom_call_target="tpu_custom_call" | custom-call | tf_op jit(solution)/shard_map/prepare/pallas_call | solution.py:386
  24.9 0.0 collective-permute-done.4.own_on
  24.9 0.0 collective-permute-done.5.own_in
  24.9 0.0 collective-permute-done.6
  24.9 3.2 %early.1 = (f32[2,2,256,256]{3,2,1,0:T(8,128)S(1)}, f32[2,2,2,256,256]{4,3,2,1,0:T(8,128)S(1)}) custom-call(s32[2,2]{1,0:T(2,128)S(4)} %get-tuple-element.18.info, f32[2,384,128]{2,1,0:T(8,128)S(1)} %get-tuple-element.19.own_o, f32[2,384,128]{2,1,0:T(8,128)S(1)} %get-tuple-element.20.own_i, f32[2,384,128]{2,1,0:T(8,128)S(1)} %collective-permute-done.4.own_on, ...), custom_call_target="tpu_custom_call" | custom-call | tf_op jit(solution)/shard_map/early/pallas_call | solution.py:404
  28.1 0.0 collective-permute-done.2.oth_on
  28.1 0.0 collective-permute-done.3.oth_in
  28.2 8.7 %grad.1 = (f32[2,384,128]{2,1,0:T(8,128)S(1)}, f32[2,384,128]{2,1,0:T(8,128)S(1)}, f32[2,384,128]{2,1,0:T(8,128)S(1)}, f32[2,384,128]{2,1,0:T(8,128)S(1)}) custom-call(s32[2,2]{1,0:T(2,128)S(4)} %get-tuple-element.18.info, f32[2,384,128]{2,1,0:T(8,128)S(1)} %collective-permute-done.oth_o, f32[2,384,128]{2,1,0:T(8,128)S(1)} %collective-permute-done.1.oth_i, ...), custom_call_target="tpu_custom_call" | custom-call | tf_op jit(solution)/shard_map/grad/pallas_call | solution.py:413
  36.8 0.6 %collective-permute-start.7 = (f32[2,384,128]{2,1,0:T(8,128)S(1)}, f32[2,384,128]{2,1,0:T(8,128)S(1)}, u32[]{:S(2)}, u32[]{:S(2)}) collective-permute-start(f32[2,384,128]{2,1,0:T(8,128)S(1)} %get-tuple-element.30), channel_id=1, source_target_pairs={{0,1},{1,0},{2,3},{3,2},{4,5},{5,4},{6,7},{7,6},{8,9},{9,8},{10,11... | collective-permute-start | bytes 1179656 | tf_op jit(solution)/shard_map/ppermute | solution.py:429
  37.4 11.2 %all-gather = f32[4,384,128]{2,1,0:T(8,128)S(1)} all-gather(f32[2,384,128]{2,1,0:T(8,128)S(1)} %get-tuple-element.29), channel_id=2, replica_groups={{1,2},{3,4},{5,6},{7,8},{9,10},{11,12},{13,14},{15,16},{17,18},{19,20},..., dimensions={0}, use_global_device_ids=true | all-gather | bytes 1179648 | tf_op jit(solution)/shard_map/all_gather | solution.py:430
  48.6 0.0 collective-permute-done.7.rb
  48.6 1.0 %merge.1 = f32[1,2,384,256]{3,2,1,0:T(8,128)} custom-call(f32[2,384,128]{2,1,0:T(8,128)S(1)} %get-tuple-element.27.a, f32[2,384,128]{2,1,0:T(8,128)S(1)} %get-tuple-element.28.b, f32[2,2,384,128]{3,2,1,0:T(8,128)S(1)} %bitcast.2, f32[2,384,128]{2,1,0:T(8,128)S(1)} %collective-permute-done.7.rb), custom_call_target="tpu_custom_call" | custom-call | tf_op jit(solution)/shard_map/merge/pallas_call | solution.py:431
Async XLA Ops:
  1.1 13.3 %collective-permute-start = (f32[2,384,128]{2,1,0:T(8,128)S(1)}, f32[2,384,128]{2,1,0:T(8,128)S(1)}, u32[]{:S(2)}, u32[]{:S(2)}) collective-permute-start(f32[2,384,128]{2,1,0:T(8,128)S(1)} %get-tuple-element.19.own_o), channel_id=1, source_target_pairs={{0,192},{192,0},{64,128},{128,64},{1,193},{193,1},{65,129},{129,65... | collective-permute-start | bytes 1179656 | tf_op jit(solution)/shard_map/ppermute | solution.py:376
  4.0 17.7 %collective-permute-start.1 = (f32[2,384,128]{2,1,0:T(8,128)S(1)}, f32[2,384,128]{2,1,0:T(8,128)S(1)}, u32[]{:S(2)}, u32[]{:S(2)}) collective-permute-start(f32[2,384,128]{2,1,0:T(8,128)S(1)} %get-tuple-element.20.own_i), channel_id=1, source_target_pairs={{0,192},{192,0},{64,128},{128,64},{1,193},{193,1},{65,129},{129,65... | collective-permute-start | bytes 1179656 | tf_op jit(solution)/shard_map/ppermute | solution.py:377
  4.5 20.4 %collective-permute-start.6 = (f32[1,2,256,256]{3,2,1,0:T(8,128)}, f32[1,2,256,256]{3,2,1,0:T(8,128)S(1)}, u32[]{:S(2)}, u32[]{:S(2)}) collective-permute-start(f32[1,2,256,256]{3,2,1,0:T(8,128)} %prb_hbm.1), channel_id=1, source_target_pairs={{0,64},{64,0},{1,65},{65,1},{2,66},{66,2},{3,67},{67,3},{4,68},{68... | collective-permute-start | bytes 1572872 | tf_op jit(solution)/shard_map/ppermute | solution.py:380
  4.7 20.1 %collective-permute-start.4 = (f32[2,384,128]{2,1,0:T(8,128)S(1)}, f32[2,384,128]{2,1,0:T(8,128)S(1)}, u32[]{:S(2)}, u32[]{:S(2)}) collective-permute-start(f32[2,384,128]{2,1,0:T(8,128)S(1)} %get-tuple-element.19.own_o), channel_id=1, source_target_pairs={{1,2},{3,4},{5,6},{7,8},{9,10},{11,12},{13,14},{15,16},{17,18},{19... | collective-permute-start | bytes 1179656 | tf_op jit(solution)/shard_map/ppermute | solution.py:378
  7.8 17.1 %collective-permute-start.5 = (f32[2,384,128]{2,1,0:T(8,128)S(1)}, f32[2,384,128]{2,1,0:T(8,128)S(1)}, u32[]{:S(2)}, u32[]{:S(2)}) collective-permute-start(f32[2,384,128]{2,1,0:T(8,128)S(1)} %get-tuple-element.20.own_i), channel_id=1, source_target_pairs={{0,1},{1,0},{2,3},{3,2},{4,5},{5,4},{6,7},{7,6},{8,9},{9,8},{10,11... | collective-permute-start | bytes 1179656 | tf_op jit(solution)/shard_map/ppermute | solution.py:379
  14.4 13.7 %collective-permute-start.2 = (f32[2,384,128]{2,1,0:T(8,128)S(1)}, f32[2,384,128]{2,1,0:T(8,128)S(1)}, u32[]{:S(2)}, u32[]{:S(2)}) collective-permute-start(f32[2,384,128]{2,1,0:T(8,128)S(1)} %collective-permute-done.oth_o), channel_id=1, source_target_pairs={{1,2},{3,4},{5,6},{7,8},{9,10},{11,12},{13,14},{15,16},{17,18},{19... | collective-permute-start | bytes 1179656 | tf_op jit(solution)/shard_map/ppermute | solution.py:381
  21.7 6.4 %collective-permute-start.3 = (f32[2,384,128]{2,1,0:T(8,128)S(1)}, f32[2,384,128]{2,1,0:T(8,128)S(1)}, u32[]{:S(2)}, u32[]{:S(2)}) collective-permute-start(f32[2,384,128]{2,1,0:T(8,128)S(1)} %collective-permute-done.1.oth_i), channel_id=1, source_target_pairs={{0,1},{1,0},{2,3},{3,2},{4,5},{5,4},{6,7},{7,6},{8,9},{9,8},{10,11... | collective-permute-start | bytes 1179656 | tf_op jit(solution)/shard_map/ppermute | solution.py:382
  21.7 0.7 %copy-start = (s32[2,2]{1,0:T(2,128)S(1)}, s32[2,2]{1,0:T(2,128)}, u32[]{:S(2)}) copy-start(s32[2,2]{1,0:T(2,128)} %where.1) | copy-start | bytes 52
  36.8 11.8 %collective-permute-start.7 = (f32[2,384,128]{2,1,0:T(8,128)S(1)}, f32[2,384,128]{2,1,0:T(8,128)S(1)}, u32[]{:S(2)}, u32[]{:S(2)}) collective-permute-start(f32[2,384,128]{2,1,0:T(8,128)S(1)} %get-tuple-element.30), channel_id=1, source_target_pairs={{0,1},{1,0},{2,3},{3,2},{4,5},{5,4},{6,7},{7,6},{8,9},{9,8},{10,11... | collective-permute-start | bytes 1179656 | tf_op jit(solution)/shard_map/ppermute | solution.py:429

commit v3 on v2

--- a/solution.py
+++ b/solution.py
@@ -48,7 +48,7 @@
     return jnp.dot(a, b, preferred_element_type=F32)
 
 
-RC = 32
+RC = 64
 LIMIT = 20 * 2**20
 
 
@@ -212,14 +212,13 @@
     acc[...] = jnp.zeros(acc.shape, F32)
     probes = (prb0, prb1)
 
-    def position(pos, carry):
+    def position(section0, pos, carry):
         def store(c, rows, at, value):
             win[c, rows, at] = value
 
         cut(info, pos, ext, store)
 
-        @pl.when(d == 0)
-        def _():
+        if section0:
             for mode in range(2):
                 for r in range(0, FULL, RC):
                     rr = pl.ds(r, RC)
@@ -227,8 +226,7 @@
                     wr, wi = win[0, rr], win[1, rr]
                     halves_to_lh(lh, mode, r, pr * wr - pi * wi, pr * wi + pi * wr)
 
-        @pl.when(d != 0)
-        def _():
+        if not section0:
             for mode in range(2):
                 for r in range(0, FULL, RC):
                     rr = pl.ds(r, RC)
@@ -287,8 +285,7 @@
             qi = jnp.concatenate([y0[:, HALF:], y1[:, HALF:]], axis=1)
             return qr, qi
 
-        @pl.when(d == 0)
-        def _():
+        if section0:
             for mode in range(2):
                 for r in range(0, FULL, RC):
                     rr = pl.ds(r, RC)
@@ -309,8 +306,7 @@
                 win[0, rr] = vr
                 win[1, rr] = vi
 
-        @pl.when(d != 0)
-        def _():
+        if not section0:
             for r in range(0, FULL, RC):
                 rr = pl.ds(r, RC)
                 vr = vi = None
@@ -337,7 +333,14 @@
                     acc[q + b, c, pl.ds(top + r, RC), :] = acc[q + b, c, pl.ds(top + r, RC), :] + vals[b]
         return carry
 
-    lax.fori_loop(0, 2, position, 0)
+    @pl.when(d == 0)
+    def _():
+        lax.fori_loop(0, 2, lambda pos, carry: position(True, pos, carry), 0)
+
+    @pl.when(d != 0)
+    def _():
+        lax.fori_loop(0, 2, lambda pos, carry: position(False, pos, carry), 0)
+
     for blk, out in ((0, g_on), (1, g_o), (2, g_i), (3, g_in)):
         out[...] = acc[blk + odd * (3 - 2 * blk)]
 

time: 50 us -> 49.2 us (0.984)
  Pallas kernels: 16.5 us -> 15.5 us
    pallas_call x1, Pallas kernels: 8.69 us -> 7.73 us  [step(): pl.pallas_call(grad, out_shape=(block,) * 4, in_specs=[smem] + [vmem] * 1...]
  transfers between devices with their start and end apart: 8 -> 8, of which waited for: 2 -> 2; matrix products, arithmetic and copies ran while one was open for 0% -> 0% of each run, Pallas kernels for 11% -> 12%
where the time goes in v3:
time: 49.2 us; the launch traced here: 48.8 us
  Pallas kernels  15.5 us (32%)
  waiting for transfers between devices  11.4 us (23%)
  blocking collectives  11.2 us (23%)
  starting transfers between devices  9.79 us (20%)
  local copies, waits for them, and re-layouts  0.68 us (1%)
    all_gather x1, blocking collectives, step(): r_o = lax.all_gather(g_on, ('mode', 'tile'), axis_index_groups=groups)  11.2 us
    pallas_call x1, Pallas kernels, step(): pl.pallas_call(grad, out_shape=(block,) * 4, in_specs=[smem] + [vmem] * 1...  7.73 us
    ppermute x1, waiting for transfers between devices, step(): oth_o = lax.ppermute(own_o, ('depth', 'mode'), cross)  5.99 us
    ppermute x1, waiting for transfers between devices, step(): oth_i = lax.ppermute(own_i, ('depth', 'mode'), cross)  5.38 us
    pallas_call x1, Pallas kernels, step(): pl.pallas_call(early, out_shape=(pair_of, pltpu.VMEM((2, 2, 2, FULL, FULL...  3.22 us
    ppermute x1, starting transfers between devices, step(): own_on = lax.ppermute(own_o, 'tile', side)  3.06 us
    ppermute x1, starting transfers between devices, step(): oth_o = lax.ppermute(own_o, ('depth', 'mode'), cross)  2.85 us
    pallas_call x1, Pallas kernels, step(): pl.pallas_call(prepare, out_shape=(pltpu.SMEM((2, 2), jnp.int32), pltpu.V...  2.46 us
  transfers between devices with their start and end apart: 8, of which 2 were waited for; matrix products, arithmetic and copies ran while one was open for 0% of the time, Pallas kernels for 12%

profile of v3, /device:TPU:128, one launch (start us, length us, event | category | flops | bytes accessed | tf_op | source)
XLA Modules:
  0.0 48.8 jit_solution(8891084774947967441)
XLA Ops:
  0.0 1.1 %halve.1 = (f32[2,384,128]{2,1,0:T(8,128)S(1)}, f32[2,384,128]{2,1,0:T(8,128)S(1)}) custom-call(f32[1,2,384,256]{3,2,1,0:T(8,128)} %whole.1), custom_call_target="tpu_custom_call" | custom-call | tf_op jit(solution)/shard_map/halve/pallas_call | solution.py:370
  1.1 2.8 %collective-permute-start = (f32[2,384,128]{2,1,0:T(8,128)S(1)}, f32[2,384,128]{2,1,0:T(8,128)S(1)}, u32[]{:S(2)}, u32[]{:S(2)}) collective-permute-start(f32[2,384,128]{2,1,0:T(8,128)S(1)} %get-tuple-element.19.own_o), channel_id=1, source_target_pairs={{0,192},{192,0},{64,128},{128,64},{1,193},{193,1},{65,129},{129,65... | collective-permute-start | bytes 1179656 | tf_op jit(solution)/shard_map/ppermute | solution.py:379
  4.0 0.5 collective-permute-start.1
  4.5 0.3 collective-permute-start.6
  4.7 3.1 %collective-permute-start.4 = (f32[2,384,128]{2,1,0:T(8,128)S(1)}, f32[2,384,128]{2,1,0:T(8,128)S(1)}, u32[]{:S(2)}, u32[]{:S(2)}) collective-permute-start(f32[2,384,128]{2,1,0:T(8,128)S(1)} %get-tuple-element.19.own_o), channel_id=1, source_target_pairs={{1,2},{3,4},{5,6},{7,8},{9,10},{11,12},{13,14},{15,16},{17,18},{19... | collective-permute-start | bytes 1179656 | tf_op jit(solution)/shard_map/ppermute | solution.py:381
  7.8 0.6 %collective-permute-start.5 = (f32[2,384,128]{2,1,0:T(8,128)S(1)}, f32[2,384,128]{2,1,0:T(8,128)S(1)}, u32[]{:S(2)}, u32[]{:S(2)}) collective-permute-start(f32[2,384,128]{2,1,0:T(8,128)S(1)} %get-tuple-element.20.own_i), channel_id=1, source_target_pairs={{0,1},{1,0},{2,3},{3,2},{4,5},{5,4},{6,7},{7,6},{8,9},{9,8},{10,11... | collective-permute-start | bytes 1179656 | tf_op jit(solution)/shard_map/ppermute | solution.py:382
  8.4 6.0 %collective-permute-done.oth_o = f32[2,384,128]{2,1,0:T(8,128)S(1)} collective-permute-done((f32[2,384,128]{2,1,0:T(8,128)S(1)}, f32[2,384,128]{2,1,0:T(8,128)S(1)}, u32[]{:S(2)}, u32[]{:S(2)}) %collective-permute-start) | collective-permute-done | bytes 393248 | tf_op jit(solution)/shard_map/ppermute | solution.py:379
  14.4 1.9 %collective-permute-start.2 = (f32[2,384,128]{2,1,0:T(8,128)S(1)}, f32[2,384,128]{2,1,0:T(8,128)S(1)}, u32[]{:S(2)}, u32[]{:S(2)}) collective-permute-start(f32[2,384,128]{2,1,0:T(8,128)S(1)} %collective-permute-done.oth_o), channel_id=1, source_target_pairs={{1,2},{3,4},{5,6},{7,8},{9,10},{11,12},{13,14},{15,16},{17,18},{19... | collective-permute-start | bytes 1179656 | tf_op jit(solution)/shard_map/ppermute | solution.py:384
  16.3 5.4 %collective-permute-done.1.oth_i = f32[2,384,128]{2,1,0:T(8,128)S(1)} collective-permute-done((f32[2,384,128]{2,1,0:T(8,128)S(1)}, f32[2,384,128]{2,1,0:T(8,128)S(1)}, u32[]{:S(2)}, u32[]{:S(2)}) %collective-permute-start.1) | collective-permute-done | bytes 393248 | tf_op jit(solution)/shard_map/ppermute | solution.py:380
  21.7 0.0 collective-permute-start.3
  21.7 0.0 copy-start
  21.7 0.7 %copy-done = s32[2,2]{1,0:T(2,128)S(1)} copy-done((s32[2,2]{1,0:T(2,128)S(1)}, s32[2,2]{1,0:T(2,128)}, u32[]{:S(2)}) %copy-start) | copy-done | bytes 40
  22.4 2.5 %prepare.1 = (s32[2,2]{1,0:T(2,128)S(4)}, f32[2,2,128,256]{3,2,1,0:T(8,128)S(1)}, bf16[8,256,256]{2,1,0:T(8,128)(2,1)S(1)}, bf16[8,256,256]{2,1,0:T(8,128)(2,1)S(1)}, f32[2,256,256]{2,1,0:T(8,128)S(1)}) custom-call(s32[2,2]{1,0:T(2,128)S(1)} %copy-done, f32[1,2,256,256]{3,2,1,0:T(8,128)} %prb_hbm.1, f32[2,256,256]{2,1,0:T(8,128)} %meas_hbm.1, ...), custom_call_target="tpu_custom_call" | custom-call | tf_op jit(solution)/shard_map/prepare/pallas_call | solution.py:389
  24.9 0.0 collective-permute-done.4.own_on
  24.9 0.0 collective-permute-done.5.own_in
  24.9 0.0 collective-permute-done.6
  24.9 3.2 %early.1 = (f32[2,2,256,256]{3,2,1,0:T(8,128)S(1)}, f32[2,2,2,256,256]{4,3,2,1,0:T(8,128)S(1)}) custom-call(s32[2,2]{1,0:T(2,128)S(4)} %get-tuple-element.18.info, f32[2,384,128]{2,1,0:T(8,128)S(1)} %get-tuple-element.19.own_o, f32[2,384,128]{2,1,0:T(8,128)S(1)} %get-tuple-element.20.own_i, f32[2,384,128]{2,1,0:T(8,128)S(1)} %collective-permute-done.4.own_on, ...), custom_call_target="tpu_custom_call" | custom-call | tf_op jit(solution)/shard_map/early/pallas_call | solution.py:407
  28.1 0.0 collective-permute-done.2.oth_on
  28.1 0.0 collective-permute-done.3.oth_in
  28.1 7.7 %grad.1 = (f32[2,384,128]{2,1,0:T(8,128)S(1)}, f32[2,384,128]{2,1,0:T(8,128)S(1)}, f32[2,384,128]{2,1,0:T(8,128)S(1)}, f32[2,384,128]{2,1,0:T(8,128)S(1)}) custom-call(s32[2,2]{1,0:T(2,128)S(4)} %get-tuple-element.18.info, f32[2,384,128]{2,1,0:T(8,128)S(1)} %collective-permute-done.oth_o, f32[2,384,128]{2,1,0:T(8,128)S(1)} %collective-permute-done.1.oth_i, ...), custom_call_target="tpu_custom_call" | custom-call | tf_op jit(solution)/shard_map/grad/pallas_call | solution.py:416
  35.9 0.6 %collective-permute-start.7 = (f32[2,384,128]{2,1,0:T(8,128)S(1)}, f32[2,384,128]{2,1,0:T(8,128)S(1)}, u32[]{:S(2)}, u32[]{:S(2)}) collective-permute-start(f32[2,384,128]{2,1,0:T(8,128)S(1)} %get-tuple-element.30), channel_id=1, source_target_pairs={{0,1},{1,0},{2,3},{3,2},{4,5},{5,4},{6,7},{7,6},{8,9},{9,8},{10,11... | collective-permute-start | bytes 1179656 | tf_op jit(solution)/shard_map/ppermute | solution.py:432
  36.5 11.2 %all-gather = f32[4,384,128]{2,1,0:T(8,128)S(1)} all-gather(f32[2,384,128]{2,1,0:T(8,128)S(1)} %get-tuple-element.29), channel_id=2, replica_groups={{1,2},{3,4},{5,6},{7,8},{9,10},{11,12},{13,14},{15,16},{17,18},{19,20},..., dimensions={0}, use_global_device_ids=true | all-gather | bytes 1179648 | tf_op jit(solution)/shard_map/all_gather | solution.py:433
  47.7 0.0 collective-permute-done.7.rb
  47.7 1.0 %merge.1 = f32[1,2,384,256]{3,2,1,0:T(8,128)} custom-call(f32[2,384,128]{2,1,0:T(8,128)S(1)} %get-tuple-element.27.a, f32[2,384,128]{2,1,0:T(8,128)S(1)} %get-tuple-element.28.b, f32[2,2,384,128]{3,2,1,0:T(8,128)S(1)} %bitcast.2, f32[2,384,128]{2,1,0:T(8,128)S(1)} %collective-permute-done.7.rb), custom_call_target="tpu_custom_call" | custom-call | tf_op jit(solution)/shard_map/merge/pallas_call | solution.py:434
Async XLA Ops:
  1.1 13.3 %collective-permute-start = (f32[2,384,128]{2,1,0:T(8,128)S(1)}, f32[2,384,128]{2,1,0:T(8,128)S(1)}, u32[]{:S(2)}, u32[]{:S(2)}) collective-permute-start(f32[2,384,128]{2,1,0:T(8,128)S(1)} %get-tuple-element.19.own_o), channel_id=1, source_target_pairs={{0,192},{192,0},{64,128},{128,64},{1,193},{193,1},{65,129},{129,65... | collective-permute-start | bytes 1179656 | tf_op jit(solution)/shard_map/ppermute | solution.py:379
  4.0 17.7 %collective-permute-start.1 = (f32[2,384,128]{2,1,0:T(8,128)S(1)}, f32[2,384,128]{2,1,0:T(8,128)S(1)}, u32[]{:S(2)}, u32[]{:S(2)}) collective-permute-start(f32[2,384,128]{2,1,0:T(8,128)S(1)} %get-tuple-element.20.own_i), channel_id=1, source_target_pairs={{0,192},{192,0},{64,128},{128,64},{1,193},{193,1},{65,129},{129,65... | collective-permute-start | bytes 1179656 | tf_op jit(solution)/shard_map/ppermute | solution.py:380
  4.5 20.4 %collective-permute-start.6 = (f32[1,2,256,256]{3,2,1,0:T(8,128)}, f32[1,2,256,256]{3,2,1,0:T(8,128)S(1)}, u32[]{:S(2)}, u32[]{:S(2)}) collective-permute-start(f32[1,2,256,256]{3,2,1,0:T(8,128)} %prb_hbm.1), channel_id=1, source_target_pairs={{0,64},{64,0},{1,65},{65,1},{2,66},{66,2},{3,67},{67,3},{4,68},{68... | collective-permute-start | bytes 1572872 | tf_op jit(solution)/shard_map/ppermute | solution.py:383
  4.7 20.1 %collective-permute-start.4 = (f32[2,384,128]{2,1,0:T(8,128)S(1)}, f32[2,384,128]{2,1,0:T(8,128)S(1)}, u32[]{:S(2)}, u32[]{:S(2)}) collective-permute-start(f32[2,384,128]{2,1,0:T(8,128)S(1)} %get-tuple-element.19.own_o), channel_id=1, source_target_pairs={{1,2},{3,4},{5,6},{7,8},{9,10},{11,12},{13,14},{15,16},{17,18},{19... | collective-permute-start | bytes 1179656 | tf_op jit(solution)/shard_map/ppermute | solution.py:381
  7.8 17.1 %collective-permute-start.5 = (f32[2,384,128]{2,1,0:T(8,128)S(1)}, f32[2,384,128]{2,1,0:T(8,128)S(1)}, u32[]{:S(2)}, u32[]{:S(2)}) collective-permute-start(f32[2,384,128]{2,1,0:T(8,128)S(1)} %get-tuple-element.20.own_i), channel_id=1, source_target_pairs={{0,1},{1,0},{2,3},{3,2},{4,5},{5,4},{6,7},{7,6},{8,9},{9,8},{10,11... | collective-permute-start | bytes 1179656 | tf_op jit(solution)/shard_map/ppermute | solution.py:382
  14.4 13.7 %collective-permute-start.2 = (f32[2,384,128]{2,1,0:T(8,128)S(1)}, f32[2,384,128]{2,1,0:T(8,128)S(1)}, u32[]{:S(2)}, u32[]{:S(2)}) collective-permute-start(f32[2,384,128]{2,1,0:T(8,128)S(1)} %collective-permute-done.oth_o), channel_id=1, source_target_pairs={{1,2},{3,4},{5,6},{7,8},{9,10},{11,12},{13,14},{15,16},{17,18},{19... | collective-permute-start | bytes 1179656 | tf_op jit(solution)/shard_map/ppermute | solution.py:384
  21.7 6.4 %collective-permute-start.3 = (f32[2,384,128]{2,1,0:T(8,128)S(1)}, f32[2,384,128]{2,1,0:T(8,128)S(1)}, u32[]{:S(2)}, u32[]{:S(2)}) collective-permute-start(f32[2,384,128]{2,1,0:T(8,128)S(1)} %collective-permute-done.1.oth_i), channel_id=1, source_target_pairs={{0,1},{1,0},{2,3},{3,2},{4,5},{5,4},{6,7},{7,6},{8,9},{9,8},{10,11... | collective-permute-start | bytes 1179656 | tf_op jit(solution)/shard_map/ppermute | solution.py:385
  21.7 0.7 %copy-start = (s32[2,2]{1,0:T(2,128)S(1)}, s32[2,2]{1,0:T(2,128)}, u32[]{:S(2)}) copy-start(s32[2,2]{1,0:T(2,128)} %where.1) | copy-start | bytes 52
  35.9 11.8 %collective-permute-start.7 = (f32[2,384,128]{2,1,0:T(8,128)S(1)}, f32[2,384,128]{2,1,0:T(8,128)S(1)}, u32[]{:S(2)}, u32[]{:S(2)}) collective-permute-start(f32[2,384,128]{2,1,0:T(8,128)S(1)} %get-tuple-element.30), channel_id=1, source_target_pairs={{0,1},{1,0},{2,3},{3,2},{4,5},{5,4},{6,7},{7,6},{8,9},{9,8},{10,11... | collective-permute-start | bytes 1179656 | tf_op jit(solution)/shard_map/ppermute | solution.py:432
